TPU v7x, 16 devices: a 4x2x1 block of a 4x4x8 slice. The times are simulated.
16 devices in a mesh: dp: 2 (over y, z), ep: 8 (over x, core).
Axes of the slice: x: 4, y: 2, z: 1, core: 2. Of those that a mesh axis runs over, the one named last changes fastest.
The devices are a block of a 4x4x8 slice.
Arguments:
- tokens: bfloat16 [4096, 1536], P(('dp', 'ep')), parts along dimension 0
- expert_ids: int32 [4096, 6], P(('dp', 'ep')), parts along dimension 0
- gate_vals: float32 [4096, 6], P(('dp', 'ep')), parts along dimension 0
- w_gate: bfloat16 [64, 1536, 512], P('ep')
- w_up: bfloat16 [64, 1536, 512], P('ep')
- w_down: bfloat16 [64, 512, 1536], P('ep')
Outputs:
- output: bfloat16 [4096, 1536], P(('dp', 'ep')), parts along dimension 0
There are 2 independent parts. A program takes and returns all parts, laid end to end along the dimension named above; an argument that names none is the same for every part.
All inputs are finite; a program needn't handle non-finite values.
Results may differ from a plain program's by a relative error of at most 0.00663984.
Values are sent between devices in bfloat16 or wider.
A program may use at most 768 MiB of HBM per device.

v0:
```python
import jax
import jax.numpy as jnp
from jax import lax
from jax.sharding import PartitionSpec as P, NamedSharding


def expert_ffn(expert_in, w_gate, w_up, w_down):
    gate_act = jnp.einsum('lcd,ldf->lcf', expert_in, w_gate, preferred_element_type=jnp.float32)
    up_act = jnp.einsum('lcd,ldf->lcf', expert_in, w_up, preferred_element_type=jnp.float32)
    hidden = (jax.nn.silu(gate_act) * up_act).astype(jnp.bfloat16)
    return jnp.einsum('lcf,lfd->lcd', hidden, w_down, preferred_element_type=jnp.float32).astype(jnp.bfloat16)


def serve_rows(recv_rows, recv_gate, w_gate, w_up, w_down, expert_cap):
    member = recv_gate != 0.0
    exp_slot = jnp.cumsum(member.astype(jnp.int32), axis=0) - 1
    fan_mat = (member.T[:, None, :] & (exp_slot.T[:, None, :] == jnp.arange(expert_cap)[None, :, None])).astype(jnp.bfloat16)
    expert_in = jnp.einsum('lcr,rd->lcd', fan_mat, recv_rows, preferred_element_type=jnp.float32).astype(jnp.bfloat16)
    expert_out = expert_ffn(expert_in, w_gate, w_up, w_down)
    row_outs = jnp.einsum('lcr,lcd->lrd', fan_mat, expert_out, preferred_element_type=jnp.float32)
    dev_sum = jnp.sum(recv_gate.T[:, :, None] * row_outs, axis=0)
    return dev_sum.astype(jnp.bfloat16)


def send_tables(expert_ids, gate_vals, groups, local_count, pair_cap):
    tok_dev = expert_ids.shape[0]
    chosen = jnp.any((expert_ids // local_count)[:, :, None] == jnp.arange(groups)[None, None, :], axis=1)
    send_rank = jnp.cumsum(chosen.astype(jnp.int32), axis=0) - 1
    pack_mask = chosen.T[:, None, :] & (send_rank.T[:, None, :] == jnp.arange(pair_cap)[None, :, None])
    gate_dense = jnp.sum(jnp.where(expert_ids[:, :, None] == jnp.arange(groups * local_count)[None, None, :], gate_vals[:, :, None], 0.0), axis=1)
    gate_t = jnp.swapaxes(gate_dense.reshape(tok_dev, groups, local_count), 0, 1)
    send_gate = jnp.sum(jnp.where(pack_mask[:, :, :, None], gate_t[:, None, :, :], 0.0), axis=2)
    return pack_mask.astype(jnp.bfloat16), send_gate


def solution(mesh):
    groups = mesh.shape['ep']
    row_spec = P(('dp', 'ep'))
    expert_spec = P('ep')

    def device_step(tokens, expert_ids, gate_vals, w_gate, w_up, w_down):
        tok_dev, top_k = expert_ids.shape
        d_model = tokens.shape[1]
        local_count = w_gate.shape[0]
        pair_cap = tok_dev * (top_k // 2) // groups
        expert_cap = tok_dev * top_k // local_count
        row_count = groups * pair_cap
        pack_mat, send_gate = send_tables(expert_ids, gate_vals, groups, local_count, pair_cap)
        send_rows = jnp.einsum('qct,td->qcd', pack_mat, tokens, preferred_element_type=jnp.float32).astype(jnp.bfloat16)
        recv_rows = lax.all_to_all(send_rows, 'ep', 0, 0, tiled=True)
        recv_gate = lax.all_to_all(send_gate, 'ep', 0, 0, tiled=True)
        dev_sum = serve_rows(recv_rows.reshape(row_count, d_model), recv_gate.reshape(row_count, local_count), w_gate, w_up, w_down, expert_cap)
        returned = lax.all_to_all(dev_sum.reshape(groups, pair_cap, d_model), 'ep', 0, 0, tiled=True)
        moe_sum = jnp.einsum('qct,qcd->td', pack_mat, returned, preferred_element_type=jnp.float32)
        return (tokens.astype(jnp.float32) + moe_sum).astype(jnp.bfloat16)

    return jax.shard_map(device_step, mesh=mesh, in_specs=(row_spec, row_spec, row_spec, expert_spec, expert_spec, expert_spec), out_specs=row_spec, check_vma=False)
```

profile of v0, /device:TPU:112, one launch (start us, length us, event | category | flops | bytes accessed | tf_op | source)
XLA Modules:
  0.0 108.8 jit_solution(15754992903458211965)
XLA Ops:
  0.0 0.7 add_select_fusion
  0.7 0.6 reduce-window.14
  1.3 0.2 slice_reduce_fusion
  1.7 0.8 select_reduce_fusion.1
  2.4 0.1 fusion.17
  2.6 1.0 select_reduce_fusion
  3.6 0.8 copy.31
  4.3 5.3 %all-to-all-start = ((f32[8,96,8]{1,2,0:T(8,128)}), f32[8,96,8]{1,2,0:T(8,128)S(1)}, u32[]{:S(2)}, u32[]{:S(2)}) async-start(f32[8,96,8]{1,2,0:T(8,128)} %copy.31), calls=%async_computation | async-start | bytes 65536 | tf_op jit(solution)/shard_map/all_to_all | solution.py:51
  9.6 3.3 %convolution_convert_fusion = bf16[8,96,1536]{2,1,0:T(8,128)(2,1)} fusion(bf16[256,1536]{1,0:T(8,128)(2,1)} %param.6, s32[8,256]{1,0:T(8,128)S(1)} %add_bitcast_fusion.1, pred[8,256]{1,0:T(8,128)(4,1)S(1)} %bitcast.47), kind=kOutput, calls=%fused_computation.8 | convolution fusion | flops 605552640 | bytes 3155968 | tf_op jit(solution)/shard_map/qct,td->qcd/dot_general | solution.py:49
  13.0 1.9 %all-to-all-done = f32[8,96,8]{1,2,0:T(8,128)S(1)} async-done(((f32[8,96,8]{1,2,0:T(8,128)}), f32[8,96,8]{1,2,0:T(8,128)S(1)}, u32[]{:S(2)}, u32[]{:S(2)}) %all-to-all-start) | async-done | bytes 24608 | tf_op jit(solution)/shard_map/all_to_all | solution.py:51
  14.9 3.8 %all-to-all-start.1 = ((bf16[8,96,1536]{2,1,0:T(8,128)(2,1)}), bf16[8,96,1536]{2,1,0:T(8,128)(2,1)S(1)}, u32[]{:S(2)}, u32[]{:S(2)}) async-start(bf16[8,96,1536]{2,1,0:T(8,128)(2,1)} %convolution_convert_fusion), calls=%async_computation.1 | async-start | bytes 4718592 | tf_op jit(solution)/shard_map/all_to_all | solution.py:50
  18.7 0.1 reshape.58
  18.8 1.7 %reduce-window.16 = s32[8,6,128]{2,0,1:T(8,128)S(1)} reduce-window(s32[8,6,128]{2,0,1:T(8,128)S(1)} %get-tuple-element.5, s32[]{:T(128)} %constant.27.clone.1), window={size=1x1x128 pad=0_0x0_0x127_0}, to_apply=%region_5.6 | reduce-window | flops 780288 | bytes 49156 | tf_op jit(solution)/shard_map/reduce-window.2
  20.6 0.1 copy.33
  20.7 0.2 reduce-window.19
  20.9 0.1 copy.34
  21.0 0.1 add_bitcast_fusion
  21.0 27.4 %all-to-all-done.1 = bf16[8,96,1536]{2,1,0:T(8,128)(2,1)S(1)} async-done(((bf16[8,96,1536]{2,1,0:T(8,128)(2,1)}), bf16[8,96,1536]{2,1,0:T(8,128)(2,1)S(1)}, u32[]{:S(2)}, u32[]{:S(2)}) %all-to-all-start.1) | async-done | bytes 2359328 | tf_op jit(solution)/shard_map/all_to_all | solution.py:50
  48.5 4.0 %fusion.5 = bf16[8,192,1536]{2,1,0:T(8,128)(2,1)S(1)} fusion(bf16[768,1536,1]{1,0,2:T(8,128)(2,1)S(1)} %bitcast.42, s32[8,768]{1,0:T(8,128)S(1)} %add_bitcast_fusion, pred[8,768]{1,0:T(8,128)(4,1)S(1)} %get-tuple-element.6), kind=kOutput, calls=%fused_computation.6 | convolution fusion | flops 3628597248 | bytes 7108608 | tf_op jit(solution)/shard_map/lcr,rd->lcd/dot_general | solution.py:18
  52.5 6.2 %fusion.23 = f32[8,192,512]{2,1,0:T(8,128)S(1)} fusion(bf16[8,192,1536]{2,1,0:T(8,128)(2,1)S(1)} %fusion.5, bf16[8,1536,512]{2,1,0:T(8,128)(2,1)} %param.9), kind=kOutput, calls=%fused_computation.37 | convolution fusion | flops 2415919104 | bytes 20447232 | tf_op jit(solution)/shard_map/lcd,ldf->lcf/dot_general | solution.py:8
  58.7 3.9 %multiply_convert_fusion = bf16[8,192,512]{2,1,0:T(8,128)(2,1)} fusion(f32[8,192,512]{2,1,0:T(8,128)S(1)} %fusion.23, bf16[8,192,1536]{2,1,0:T(8,128)(2,1)S(1)} %fusion.5, bf16[8,1536,512]{2,1,0:T(8,128)(2,1)S(1)} %bitcast.52), kind=kOutput, calls=%fused_computation.9 | convolution fusion | flops 2420637696 | bytes 22020096 | tf_op jit(solution)/shard_map/lcd,ldf->lcf/dot_general | solution.py:9
  62.7 11.6 %multiply_reduce_fusion = bf16[768,1536]{1,0:T(8,128)(2,1)S(1)} fusion(f32[8,768]{1,0:T(8,128)S(1)} %bitcast.45, bf16[8,192,512]{2,1,0:T(8,128)(2,1)} %multiply_convert_fusion, bf16[8,512,1536]{2,1,0:T(8,128)(2,1)} %param.11, s32[8,768]{1,0:T(8,128)S(1)} %add_bitcast_fusion, pred[8,768]{1,0:T(8,128)(4,1)S(1)} %get-tuple-element.6), kind=kOutput, calls=%fused_computation | convolution fusion | flops 6062211072 | bytes 16570368 | tf_op jit(solution)/shard_map/lcr,lcd->lrd/dot_general | solution.py:20
  74.3 32.8 %all_to_all.15 = bf16[8,96,1536]{2,1,0:T(8,128)(2,1)S(1)} all-to-all(bf16[8,96,1536]{2,1,0:T(8,128)(2,1)S(1)} %bitcast.43), channel_id=1, replica_groups=mesh['dp'=2,'ep'=8] {'ep'}, dimensions={0} | all-to-all | bytes 4718592 | tf_op jit(solution)/shard_map/all_to_all | solution.py:53
  107.1 1.7 %fusion.11 = bf16[256,1536]{1,0:T(8,128)(2,1)} fusion(bf16[8,96,1536]{2,1,0:T(8,128)(2,1)S(1)} %all_to_all.15, bf16[256,1536]{1,0:T(8,128)(2,1)S(1)} %copy-done, s32[8,256]{1,0:T(8,128)S(1)} %add_bitcast_fusion.1, pred[8,256]{1,0:T(8,128)(4,1)S(1)} %bitcast.48), kind=kOutput, calls=%fused_computation.12 | convolution fusion | flops 605552640 | bytes 3942400 | tf_op jit(solution)/shard_map/qct,qcd->td/dot_general | solution.py:54
  (17 shorter events, 0.3 us)
Async XLA Ops:
  4.3 10.5 %all-to-all-start = ((f32[8,96,8]{1,2,0:T(8,128)}), f32[8,96,8]{1,2,0:T(8,128)S(1)}, u32[]{:S(2)}, u32[]{:S(2)}) async-start(f32[8,96,8]{1,2,0:T(8,128)} %copy.31), calls=%async_computation | async-start | bytes 65536 | tf_op jit(solution)/shard_map/all_to_all | solution.py:51
  14.9 33.6 %all-to-all-start.1 = ((bf16[8,96,1536]{2,1,0:T(8,128)(2,1)}), bf16[8,96,1536]{2,1,0:T(8,128)(2,1)S(1)}, u32[]{:S(2)}, u32[]{:S(2)}) async-start(bf16[8,96,1536]{2,1,0:T(8,128)(2,1)} %convolution_convert_fusion), calls=%async_computation.1 | async-start | bytes 4718592 | tf_op jit(solution)/shard_map/all_to_all | solution.py:50
  48.5 10.2 %slice-start = ((s8[12582912]{0:T(1024)(128)(4,1)}), s8[4194304]{0:T(1024)(128)(4,1)S(1)}, s32[]{:S(2)}) async-start(s8[12582912]{0:T(1024)(128)(4,1)} %bitcast.51), calls=%async_computation.3 | async-start | bytes 8388608
  48.5 10.2 %slice-start.1 = ((s8[12582912]{0:T(1024)(128)(4,1)}), s8[4194304]{0:T(1024)(128)(4,1)S(1)}, s32[]{:S(2)}) async-start(s8[12582912]{0:T(1024)(128)(4,1)} %bitcast.51), calls=%async_computation.4 | async-start | bytes 8388608
  52.5 6.2 %slice-start.2 = ((s8[12582912]{0:T(1024)(128)(4,1)}), s8[4194304]{0:T(1024)(128)(4,1)S(1)}, s32[]{:S(2)}) async-start(s8[12582912]{0:T(1024)(128)(4,1)} %bitcast.51), calls=%async_computation.5 | async-start | bytes 8388608
  74.3 32.8 %copy-start = (bf16[256,1536]{1,0:T(8,128)(2,1)S(1)}, bf16[256,1536]{1,0:T(8,128)(2,1)}, u32[]{:S(2)}) copy-start(bf16[256,1536]{1,0:T(8,128)(2,1)} %param.6) | copy-start | bytes 2359300
where the time goes:
time: 109 us
  blocking collectives  32.8 us (30%)
  matrix products  30.8 us (28%)
  waiting for transfers between devices  29.3 us (27%)
  starting transfers between devices  9.12 us (8%)
  other arithmetic  5.28 us (5%)
  local copies, waits for them, and re-layouts  1.38 us (1%)
    all_to_all x1, blocking collectives, device_step(): lax.all_to_all(dev_sum.reshape(groups, pair_cap, d_model), 'ep', 0, 0, ti...  32.8 us
    all_to_all x1, waiting for transfers between devices, device_step(): recv_rows = lax.all_to_all(send_rows, 'ep', 0, 0, tiled=True)  27.4 us
    dot_general x1, matrix products, serve_rows(): jnp.einsum('lcr,lcd->lrd', fan_mat, expert_out, preferred_element_type=jn...  11.6 us
    dot_general x1, matrix products, expert_ffn(): jnp.einsum('lcd,ldf->lcf', expert_in, w_gate, preferred_element_type=jnp....  6.17 us
    all_to_all x1, starting transfers between devices, device_step(): recv_gate = lax.all_to_all(send_gate, 'ep', 0, 0, tiled=True)  5.3 us
    dot_general x1, matrix products, serve_rows(): jnp.einsum('lcr,rd->lcd', fan_mat, recv_rows, preferred_element_type=jnp....  4 us
    dot_general x1, matrix products, expert_ffn(): jnp.einsum('lcd,ldf->lcf', expert_in, w_up, preferred_element_type=jnp.fl...  3.94 us
    all_to_all x1, starting transfers between devices, device_step(): recv_rows = lax.all_to_all(send_rows, 'ep', 0, 0, tiled=True)  3.82 us
  transfers between devices with their start and end apart: 2, of which 2 were waited for; matrix products, arithmetic and copies ran while one was open for 5% of the time, Pallas kernels for 0%

commit v1 on v0

v1 whole, which is shorter than its diff:
```python
import functools

import jax
import jax.numpy as jnp
from jax import lax
from jax.experimental import pallas as pl
from jax.experimental.pallas import tpu as pltpu
from jax.sharding import PartitionSpec as P

MESH = pl.DeviceIdType.MESH
CORES = 2


def moe_kernel(groups, cap, x_ref, ids_ref, gates_ref, wg_hbm, wu_hbm, wd_hbm, out_ref,
               wg, wu, wd, chosen, pack, send, sgate, recv, rgate, gcol, hid, acc, ysend, yrecv, total,
               wsem, send_sem, recv_sem, gsend_sem, grecv_sem, ysend_sem, yrecv_sem):
    tok_dev, d_model = x_ref.shape
    local, _, ffn = wg.shape
    top_k = ids_ref.shape[0]
    lanes = sgate.shape[2]
    chips = groups // CORES
    f32, bf16 = jnp.float32, jnp.bfloat16
    me = lax.axis_index('ep')
    chip, core = me // CORES, me % CORES
    slots = [(0, 0), (0, 1)]
    near = [(d, 0) for d in (1, chips - 1)]
    far = [(d, c) for d in range(2, chips - 1) for c in range(CORES)]
    slots += near + far + [(d, 1) for d, _ in near]

    def peer(k, sign):
        dx, dc = slots[k]
        return lax.rem(chip + chips + sign * dx, chips) * CORES + lax.rem(core + dc, CORES)

    def weight_copies(e):
        return [pltpu.make_async_copy(src.at[e], dst.at[e], wsem.at[i, e])
                for i, (src, dst) in enumerate(((wg_hbm, wg), (wu_hbm, wu), (wd_hbm, wd)))]

    for e in range(local):
        for copy in weight_copies(e):
            copy.start()

    barrier = pltpu.get_barrier_semaphore()
    for k in range(1, groups):
        pl.semaphore_signal(barrier, inc=1, device_id={'ep': peer(k, 1)}, device_id_type=MESH)

    def rows(k):
        return pl.ds(k * cap, cap)

    def row_copy(k):
        return pltpu.make_async_remote_copy(
            src_ref=send.at[rows(k), :], dst_ref=recv.at[rows(k), :], send_sem=send_sem.at[k], recv_sem=recv_sem.at[k],
            device_id={'ep': peer(k, 1)}, device_id_type=MESH)

    def gate_copy(k):
        return pltpu.make_async_remote_copy(
            src_ref=sgate.at[k], dst_ref=rgate.at[k], send_sem=gsend_sem.at[k], recv_sem=grecv_sem.at[k],
            device_id={'ep': peer(k, 1)}, device_id_type=MESH)

    def back_copy(k):
        return pltpu.make_async_remote_copy(
            src_ref=ysend.at[rows(k), :], dst_ref=yrecv.at[rows(k), :], send_sem=ysend_sem.at[k], recv_sem=yrecv_sem.at[k],
            device_id={'ep': peer(k, -1)}, device_id_type=MESH)

    ids = ids_ref[...]
    gates = gates_ref[...]
    dev = ids // local
    for k in range(groups):
        chosen[k:k + 1, :] = jnp.max(jnp.where(dev == peer(k, 1), 1.0, 0.0), axis=0, keepdims=True)
    flags = chosen[...]
    earlier = lax.broadcasted_iota(jnp.int32, (tok_dev, tok_dev), 0) < lax.broadcasted_iota(jnp.int32, (tok_dev, tok_dev), 1)
    rank = jnp.dot(flags.astype(bf16), jnp.where(earlier, 1.0, 0.0).astype(bf16), preferred_element_type=f32)
    rank = jnp.where(flags > 0.0, rank, -1.0).astype(jnp.int32)
    row_id = lax.broadcasted_iota(jnp.int32, (lanes, tok_dev), 0)
    loc_id = lax.broadcasted_iota(jnp.int32, (local, tok_dev), 0)
    order = list(range(2, groups)) + [1, 0]
    for n, k in enumerate(order):
        onehot = jnp.where(row_id == rank[k:k + 1, :], 1.0, 0.0).astype(bf16)
        pack[rows(k), :] = onehot[:cap, :]
        packed = jnp.dot(onehot[:cap, :], x_ref[...], preferred_element_type=f32).astype(bf16)
        first = peer(k, 1) * local
        gate = jnp.zeros((local, tok_dev), f32)
        for j in range(top_k):
            gate += jnp.where(ids[j:j + 1, :] - first == loc_id, gates[j:j + 1, :], 0.0)
        high = gate.astype(bf16).astype(f32)
        mid = (gate - high).astype(bf16).astype(f32)
        low = gate - high - mid
        parts = jnp.concatenate([high, mid, low], axis=0).astype(bf16)
        moved = lax.dot_general(parts, onehot, (((1,), (1,)), ((), ())), preferred_element_type=f32)
        moved = moved[:local] + moved[local:2 * local] + moved[2 * local:]
        if k == 0:
            recv[rows(k), :] = packed
            rgate[k] = moved
        else:
            send[rows(k), :] = packed
            sgate[k] = moved
            if n == 0:
                pl.semaphore_wait(barrier, groups - 1)
            gate_copy(k).start()
            row_copy(k).start()

    pair = 2 * cap
    half = ffn // 2
    third = d_model // 3
    lane_id = lax.broadcasted_iota(jnp.int32, (pair, lanes), 1)

    def batch(b, carry):
        for i in range(groups // 2):
            @pl.when(b == i)
            def _(i=i):
                for k in (2 * i, 2 * i + 1):
                    if k > 0:
                        gate_copy(k).wait_recv()
                        row_copy(k).wait_recv()
                    gcol[(k % 2) * cap:(k % 2 + 1) * cap, :] = jnp.concatenate(
                        [rgate[k], jnp.zeros((lanes - local, lanes), f32)], axis=0).T[:cap, :]
        base = pl.multiple_of(b * pair, pair)

        def hidden(e):
            @pl.when(b == 0)
            def _():
                for copy in weight_copies(e)[:2]:
                    copy.wait()
            for n in range(2):
                cols = slice(n * half, (n + 1) * half)
                g = jnp.dot(recv[pl.ds(base, pair), :], wg[e, :, cols], preferred_element_type=f32)
                u = jnp.dot(recv[pl.ds(base, pair), :], wu[e, :, cols], preferred_element_type=f32)
                hid[lax.rem(e, 2), :, cols] = (jax.nn.silu(g) * u).astype(bf16)

        def wait_down(e):
            @pl.when(b == 0)
            def _():
                weight_copies(e)[2].wait()

        def down(e):
            gate = jnp.sum(jnp.where(lane_id == e, gcol[...], 0.0), axis=1, keepdims=True)
            for n in range(3):
                cols = slice(n * third, (n + 1) * third)
                y = jnp.dot(hid[lax.rem(e, 2)], wd[e, :, cols], preferred_element_type=f32).astype(bf16).astype(f32)
                acc[:, cols] += jnp.where(gate > 0.0, gate * y, 0.0)

        acc[...] = jnp.zeros_like(acc)
        hidden(0)

        def step(e, carry):
            wait_down(e - 1)
            hidden(e)
            down(e - 1)
            return carry

        lax.fori_loop(1, local, step, 0)
        wait_down(local - 1)
        down(local - 1)
        for i in range(groups // 2):
            @pl.when(b == i)
            def _(i=i):
                for k in (2 * i, 2 * i + 1):
                    part = acc[(k % 2) * cap:(k % 2 + 1) * cap, :].astype(bf16)
                    if k == 0:
                        yrecv[rows(k), :] = part
                    else:
                        ysend[rows(k), :] = part
                        back_copy(k).start()
        return carry

    lax.fori_loop(0, groups // 2, batch, 0)

    for i in range(groups // 2):
        for k in (2 * i, 2 * i + 1):
            if k > 0:
                back_copy(k).wait_recv()
        span = slice(i * pair, (i + 1) * pair)
        part = lax.dot_general(pack[span, :], yrecv[span, :], (((0,), (0,)), ((), ())), preferred_element_type=f32)
        if i == 0:
            total[...] = x_ref[...].astype(f32) + part
        elif i < groups // 2 - 1:
            total[...] += part
        else:
            out_ref[...] = (total[...] + part).astype(bf16)
    for k in range(1, groups):
        gate_copy(k).wait_send()
        row_copy(k).wait_send()
        back_copy(k).wait_send()


def solution(mesh):
    groups = mesh.shape['ep']
    row_spec = P(('dp', 'ep'))
    expert_spec = P('ep')

    def device_step(tokens, expert_ids, gate_vals, w_gate, w_up, w_down):
        tok_dev, top_k = expert_ids.shape
        d_model = tokens.shape[1]
        local, _, ffn = w_gate.shape
        cap = tok_dev * (top_k // 2) // groups
        lanes = 128
        f32, bf16 = jnp.float32, jnp.bfloat16
        vmem = pl.BlockSpec(memory_space=pltpu.VMEM)
        hbm = pl.BlockSpec(memory_space=pl.ANY)
        dma = pltpu.SemaphoreType.DMA((groups,))
        return pl.pallas_call(
            functools.partial(moe_kernel, groups, cap),
            out_shape=jax.ShapeDtypeStruct((tok_dev, d_model), bf16),
            in_specs=[vmem, vmem, vmem, hbm, hbm, hbm],
            out_specs=vmem,
            scratch_shapes=[
                pltpu.VMEM(w_gate.shape, bf16),
                pltpu.VMEM(w_up.shape, bf16),
                pltpu.VMEM(w_down.shape, bf16),
                pltpu.VMEM((groups, tok_dev), f32),
                pltpu.VMEM((groups * cap, tok_dev), bf16),
                pltpu.VMEM((groups * cap, d_model), bf16),
                pltpu.VMEM((groups, local, lanes), f32),
                pltpu.VMEM((groups * cap, d_model), bf16),
                pltpu.VMEM((groups, local, lanes), f32),
                pltpu.VMEM((2 * cap, lanes), f32),
                pltpu.VMEM((2, 2 * cap, ffn), bf16),
                pltpu.VMEM((2 * cap, d_model), f32),
                pltpu.VMEM((groups * cap, d_model), bf16),
                pltpu.VMEM((groups * cap, d_model), bf16),
                pltpu.VMEM((tok_dev, d_model), f32),
                pltpu.SemaphoreType.DMA((3, local)),
                dma, dma, dma, dma, dma, dma,
            ],
            compiler_params=pltpu.CompilerParams(collective_id=0, has_side_effects=True, vmem_limit_bytes=67043328),
        )(tokens, expert_ids.T, gate_vals.T, w_gate, w_up, w_down)

    return jax.shard_map(device_step, mesh=mesh, in_specs=(row_spec, row_spec, row_spec, expert_spec, expert_spec, expert_spec), out_specs=row_spec, check_vma=False)
```

time: 109 us -> 67.8 us (0.62)
  the two profiles are of different devices: /device:TPU:112 before, /device:TPU:113 now
where the time goes in v1:
time: 67.8 us; the launch traced here: 67.6 us
  Pallas kernels  65.6 us (97%)
  local copies, waits for them, and re-layouts  2.06 us (3%)
    pallas_call x1, Pallas kernels, device_step(): pl.pallas_call(functools.partial(moe_kernel, groups, cap), out_shape=jax....  65.6 us
    unnamed x1, local copies, waits for them, and re-layouts  2.06 us

profile of v1, /device:TPU:113, one launch (start us, length us, event | category | flops | bytes accessed | tf_op | source)
XLA Modules:
  0.0 67.6 jit_solution(14400981309875007484)
XLA Ops:
  0.0 65.6 %shard_map.64 = bf16[256,1536]{1,0:T(8,128)(2,1)} custom-call(bf16[256,1536]{1,0:T(8,128)(2,1)} %x_ref.1, s32[6,256]{1,0:T(8,128)} %bitcast.2, f32[6,256]{1,0:T(8,128)} %bitcast.3, bf16[8,1536,512]{2,1,0:T(8,128)(2,1)} %wg_hbm.1, bf16[8,1536,512]{2,1,0:T(8,128)(2,1)} %wu_hbm.1, bf16[8,512,1536]{2,1,0:T(8,128)(2,1)} %wd_hbm.1), custom_call_target="tpu_custom_call" | custom-call | tf_op jit(solution)/shard_map/pallas_call | solution.py:200
  65.6 2.1 %copy.8 = bf16[256,1536]{1,0:T(8,128)(2,1)} copy(bf16[256,1536]{1,0:T(8,128)(2,1)} %shard_map.64) | data formatting | bytes 1572864

commit v2 on v1

--- a/solution.py
+++ b/solution.py
@@ -1,3 +1,4 @@
+import contextlib
 import functools
 
 import jax
@@ -11,9 +12,13 @@
 CORES = 2
 
 
-def moe_kernel(groups, cap, x_ref, ids_ref, gates_ref, wg_hbm, wu_hbm, wd_hbm, out_ref,
-               wg, wu, wd, chosen, pack, send, sgate, recv, rgate, gcol, hid, acc, ysend, yrecv, total,
-               wsem, send_sem, recv_sem, gsend_sem, grecv_sem, ysend_sem, yrecv_sem):
+def scope(name):
+    return contextlib.nullcontext()
+
+
+def moe_kernel(groups, cap, x_hbm, ids_hbm, gates_hbm, wg_hbm, wu_hbm, wd_hbm, out_ref,
+               x_ref, ids_ref, gates_ref, wg, wu, wd, chosen, pack, send, sgate, recv, rgate, gcol, hid, acc, ysend, yrecv, total,
+               isem, wsem, send_sem, recv_sem, gsend_sem, grecv_sem, ysend_sem, yrecv_sem):
     tok_dev, d_model = x_ref.shape
     local, _, ffn = wg.shape
     top_k = ids_ref.shape[0]
@@ -22,10 +27,11 @@
     f32, bf16 = jnp.float32, jnp.bfloat16
     me = lax.axis_index('ep')
     chip, core = me // CORES, me % CORES
-    slots = [(0, 0), (0, 1)]
-    near = [(d, 0) for d in (1, chips - 1)]
-    far = [(d, c) for d in range(2, chips - 1) for c in range(CORES)]
-    slots += near + far + [(d, 1) for d, _ in near]
+    slots = [(d, c) for c in range(CORES) for d in (1, chips - 1)]
+    slots += [(d, c) for d in range(2, chips - 1) for c in range(CORES)]
+    slots += [(0, c) for c in range(CORES)]
+    own = groups - CORES
+    others = [k for k in range(groups) if k != own]
 
     def peer(k, sign):
         dx, dc = slots[k]
@@ -35,13 +41,14 @@
         return [pltpu.make_async_copy(src.at[e], dst.at[e], wsem.at[i, e])
                 for i, (src, dst) in enumerate(((wg_hbm, wg), (wu_hbm, wu), (wd_hbm, wd)))]
 
-    for e in range(local):
-        for copy in weight_copies(e):
-            copy.start()
-
     barrier = pltpu.get_barrier_semaphore()
-    for k in range(1, groups):
+    for k in others:
         pl.semaphore_signal(barrier, inc=1, device_id={'ep': peer(k, 1)}, device_id_type=MESH)
+
+    inputs = [pltpu.make_async_copy(src, dst, isem.at[i])
+              for i, (src, dst) in enumerate(((ids_hbm, ids_ref), (gates_hbm, gates_ref), (x_hbm, x_ref)))]
+    for copy in inputs:
+        copy.start()
 
     def rows(k):
         return pl.ds(k * cap, cap)
@@ -61,6 +68,8 @@
             src_ref=ysend.at[rows(k), :], dst_ref=yrecv.at[rows(k), :], send_sem=ysend_sem.at[k], recv_sem=yrecv_sem.at[k],
             device_id={'ep': peer(k, -1)}, device_id_type=MESH)
 
+    inputs[0].wait()
+    inputs[1].wait()
     ids = ids_ref[...]
     gates = gates_ref[...]
     dev = ids // local
@@ -72,8 +81,12 @@
     rank = jnp.where(flags > 0.0, rank, -1.0).astype(jnp.int32)
     row_id = lax.broadcasted_iota(jnp.int32, (lanes, tok_dev), 0)
     loc_id = lax.broadcasted_iota(jnp.int32, (local, tok_dev), 0)
-    order = list(range(2, groups)) + [1, 0]
-    for n, k in enumerate(order):
+    inputs[2].wait()
+    for e in range(local):
+        for copy in weight_copies(e):
+            copy.start()
+
+    for n, k in enumerate(others + [own]):
         onehot = jnp.where(row_id == rank[k:k + 1, :], 1.0, 0.0).astype(bf16)
         pack[rows(k), :] = onehot[:cap, :]
         packed = jnp.dot(onehot[:cap, :], x_ref[...], preferred_element_type=f32).astype(bf16)
@@ -87,14 +100,15 @@
         parts = jnp.concatenate([high, mid, low], axis=0).astype(bf16)
         moved = lax.dot_general(parts, onehot, (((1,), (1,)), ((), ())), preferred_element_type=f32)
         moved = moved[:local] + moved[local:2 * local] + moved[2 * local:]
-        if k == 0:
+        if k == own:
             recv[rows(k), :] = packed
             rgate[k] = moved
         else:
             send[rows(k), :] = packed
             sgate[k] = moved
             if n == 0:
-                pl.semaphore_wait(barrier, groups - 1)
+                with scope('barrier'):
+                    pl.semaphore_wait(barrier, groups - 1)
             gate_copy(k).start()
             row_copy(k).start()
 
@@ -108,28 +122,20 @@
             @pl.when(b == i)
             def _(i=i):
                 for k in (2 * i, 2 * i + 1):
-                    if k > 0:
-                        gate_copy(k).wait_recv()
-                        row_copy(k).wait_recv()
+                    if k != own:
+                        with scope('rwait%d' % k):
+                            gate_copy(k).wait_recv()
+                            row_copy(k).wait_recv()
                     gcol[(k % 2) * cap:(k % 2 + 1) * cap, :] = jnp.concatenate(
                         [rgate[k], jnp.zeros((lanes - local, lanes), f32)], axis=0).T[:cap, :]
         base = pl.multiple_of(b * pair, pair)
 
         def hidden(e):
-            @pl.when(b == 0)
-            def _():
-                for copy in weight_copies(e)[:2]:
-                    copy.wait()
             for n in range(2):
                 cols = slice(n * half, (n + 1) * half)
                 g = jnp.dot(recv[pl.ds(base, pair), :], wg[e, :, cols], preferred_element_type=f32)
                 u = jnp.dot(recv[pl.ds(base, pair), :], wu[e, :, cols], preferred_element_type=f32)
                 hid[lax.rem(e, 2), :, cols] = (jax.nn.silu(g) * u).astype(bf16)
-
-        def wait_down(e):
-            @pl.when(b == 0)
-            def _():
-                weight_copies(e)[2].wait()
 
         def down(e):
             gate = jnp.sum(jnp.where(lane_id == e, gcol[...], 0.0), axis=1, keepdims=True)
@@ -138,48 +144,56 @@
                 y = jnp.dot(hid[lax.rem(e, 2)], wd[e, :, cols], preferred_element_type=f32).astype(bf16).astype(f32)
                 acc[:, cols] += jnp.where(gate > 0.0, gate * y, 0.0)
 
-        acc[...] = jnp.zeros_like(acc)
-        hidden(0)
+        with scope('first'):
+            acc[...] = jnp.zeros_like(acc)
+            hidden(0)
 
         def step(e, carry):
-            wait_down(e - 1)
             hidden(e)
             down(e - 1)
             return carry
 
-        lax.fori_loop(1, local, step, 0)
-        wait_down(local - 1)
-        down(local - 1)
+        with scope('steps'):
+            lax.fori_loop(1, local, step, 0, unroll=True)
+        with scope('last'):
+            down(local - 1)
         for i in range(groups // 2):
             @pl.when(b == i)
             def _(i=i):
                 for k in (2 * i, 2 * i + 1):
                     part = acc[(k % 2) * cap:(k % 2 + 1) * cap, :].astype(bf16)
-                    if k == 0:
+                    if k == own:
                         yrecv[rows(k), :] = part
                     else:
                         ysend[rows(k), :] = part
                         back_copy(k).start()
         return carry
 
+    for e in range(local):
+        for copy in weight_copies(e):
+            copy.wait()
     lax.fori_loop(0, groups // 2, batch, 0)
 
-    for i in range(groups // 2):
+    tail = list(range(groups // 2))
+    tail[-2:] = tail[:-3:-1]
+    for n, i in enumerate(tail):
         for k in (2 * i, 2 * i + 1):
-            if k > 0:
-                back_copy(k).wait_recv()
+            if k != own:
+                with scope('ywait%d' % k):
+                    back_copy(k).wait_recv()
         span = slice(i * pair, (i + 1) * pair)
         part = lax.dot_general(pack[span, :], yrecv[span, :], (((0,), (0,)), ((), ())), preferred_element_type=f32)
-        if i == 0:
+        if n == 0:
             total[...] = x_ref[...].astype(f32) + part
-        elif i < groups // 2 - 1:
+        elif n < len(tail) - 1:
             total[...] += part
         else:
             out_ref[...] = (total[...] + part).astype(bf16)
-    for k in range(1, groups):
-        gate_copy(k).wait_send()
-        row_copy(k).wait_send()
-        back_copy(k).wait_send()
+    with scope('sends'):
+        for k in others:
+            gate_copy(k).wait_send()
+            row_copy(k).wait_send()
+            back_copy(k).wait_send()
 
 
 def solution(mesh):
@@ -199,10 +213,13 @@
         dma = pltpu.SemaphoreType.DMA((groups,))
         return pl.pallas_call(
             functools.partial(moe_kernel, groups, cap),
-            out_shape=jax.ShapeDtypeStruct((tok_dev, d_model), bf16),
-            in_specs=[vmem, vmem, vmem, hbm, hbm, hbm],
+            out_shape=pltpu.VMEM((tok_dev, d_model), bf16),
+            in_specs=[hbm] * 6,
             out_specs=vmem,
             scratch_shapes=[
+                pltpu.VMEM(tokens.shape, bf16),
+                pltpu.VMEM((top_k, tok_dev), jnp.int32),
+                pltpu.VMEM((top_k, tok_dev), f32),
                 pltpu.VMEM(w_gate.shape, bf16),
                 pltpu.VMEM(w_up.shape, bf16),
                 pltpu.VMEM(w_down.shape, bf16),
@@ -218,10 +235,11 @@
                 pltpu.VMEM((groups * cap, d_model), bf16),
                 pltpu.VMEM((groups * cap, d_model), bf16),
                 pltpu.VMEM((tok_dev, d_model), f32),
+                pltpu.SemaphoreType.DMA((3,)),
                 pltpu.SemaphoreType.DMA((3, local)),
                 dma, dma, dma, dma, dma, dma,
             ],
-            compiler_params=pltpu.CompilerParams(collective_id=0, has_side_effects=True, vmem_limit_bytes=67043328),
+            compiler_params=pltpu.CompilerParams(collective_id=0, has_side_effects=True, vmem_limit_bytes=54 * 1024 * 1024),
         )(tokens, expert_ids.T, gate_vals.T, w_gate, w_up, w_down)
 
     return jax.shard_map(device_step, mesh=mesh, in_specs=(row_spec, row_spec, row_spec, expert_spec, expert_spec, expert_spec), out_specs=row_spec, check_vma=False)

time: 67.8 us -> 59.6 us (0.88)
  the two profiles are of different devices: /device:TPU:113 before, /device:TPU:112 now
where the time goes in v2:
time: 59.6 us; the launch traced here: 58.5 us
  Pallas kernels  57.6 us (97%)
  local copies, waits for them, and re-layouts  0.88 us (1%)
    pallas_call x1, Pallas kernels, device_step(): pl.pallas_call(functools.partial(moe_kernel, groups, cap), out_shape=pltp...  57.6 us

profile of v2, /device:TPU:112, one launch (start us, length us, event | category | flops | bytes accessed | tf_op | source)
XLA Modules:
  0.0 58.5 jit_solution(11380722881349359903)
XLA Ops:
  0.0 57.6 %shard_map.64 = bf16[256,1536]{1,0:T(8,128)(2,1)S(1)} custom-call(bf16[256,1536]{1,0:T(8,128)(2,1)} %x_hbm.1, s32[6,256]{1,0:T(8,128)} %bitcast.2, f32[6,256]{1,0:T(8,128)} %bitcast.3, bf16[8,1536,512]{2,1,0:T(8,128)(2,1)} %wg_hbm.1, bf16[8,1536,512]{2,1,0:T(8,128)(2,1)} %wu_hbm.1, bf16[8,512,1536]{2,1,0:T(8,128)(2,1)} %wd_hbm.1), custom_call_target="tpu_custom_call" | custom-call | tf_op jit(solution)/shard_map/pallas_call | solution.py:214
  57.6 0.9 %copy.8 = bf16[256,1536]{1,0:T(8,128)(2,1)} copy(bf16[256,1536]{1,0:T(8,128)(2,1)S(1)} %shard_map.64) | data formatting | bytes 1572864

commit v3 on v2

--- a/solution.py
+++ b/solution.py
@@ -17,8 +17,8 @@
 
 
 def moe_kernel(groups, cap, x_hbm, ids_hbm, gates_hbm, wg_hbm, wu_hbm, wd_hbm, out_ref,
-               x_ref, ids_ref, gates_ref, wg, wu, wd, chosen, pack, send, sgate, recv, rgate, gcol, hid, acc, ysend, yrecv, total,
-               isem, wsem, send_sem, recv_sem, gsend_sem, grecv_sem, ysend_sem, yrecv_sem):
+               x_ref, ids_ref, gates_ref, wg, wu, wd, chosen, rank, rrank, raw, pack, send, sgate, recv, rgate, gcol, hid, acc, ysend, yrecv, total,
+               isem, wsem, raw_sem, send_sem, recv_sem, gsend_sem, grecv_sem, ysend_sem, yrecv_sem):
     tok_dev, d_model = x_ref.shape
     local, _, ffn = wg.shape
     top_k = ids_ref.shape[0]
@@ -27,15 +27,14 @@
     f32, bf16 = jnp.float32, jnp.bfloat16
     me = lax.axis_index('ep')
     chip, core = me // CORES, me % CORES
-    slots = [(d, c) for c in range(CORES) for d in (1, chips - 1)]
-    slots += [(d, c) for d in range(2, chips - 1) for c in range(CORES)]
-    slots += [(0, c) for c in range(CORES)]
-    own = groups - CORES
+    side = 1 - 2 * core
+    dests = [(side, 0), (side, 1), (-side, 0), (chips // 2, 0), (-side, 1), (chips // 2, 1), (0, 0), (0, 1)]
+    homes = [(-side, 0), (side, 1), (side, 0), (chips // 2, 0), (-side, 1), (chips // 2, 1), (0, 0), (0, 1)]
+    direct, relayed, own = (2, 4), (1, 3, 5), 6
     others = [k for k in range(groups) if k != own]
 
-    def peer(k, sign):
-        dx, dc = slots[k]
-        return lax.rem(chip + chips + sign * dx, chips) * CORES + lax.rem(core + dc, CORES)
+    def device(dx, dc):
+        return lax.rem(chip + chips + dx, chips) * CORES + lax.rem(core + dc, CORES)
 
     def weight_copies(e):
         return [pltpu.make_async_copy(src.at[e], dst.at[e], wsem.at[i, e])
@@ -43,7 +42,7 @@
 
     barrier = pltpu.get_barrier_semaphore()
     for k in others:
-        pl.semaphore_signal(barrier, inc=1, device_id={'ep': peer(k, 1)}, device_id_type=MESH)
+        pl.semaphore_signal(barrier, inc=1, device_id={'ep': device(*dests[k])}, device_id_type=MESH)
 
     inputs = [pltpu.make_async_copy(src, dst, isem.at[i])
               for i, (src, dst) in enumerate(((ids_hbm, ids_ref), (gates_hbm, gates_ref), (x_hbm, x_ref)))]
@@ -53,20 +52,27 @@
     def rows(k):
         return pl.ds(k * cap, cap)
 
+    def remote(src, dst, sems, to):
+        return pltpu.make_async_remote_copy(
+            src_ref=src, dst_ref=dst, send_sem=sems[0], recv_sem=sems[1], device_id={'ep': device(*to)}, device_id_type=MESH)
+
     def row_copy(k):
-        return pltpu.make_async_remote_copy(
-            src_ref=send.at[rows(k), :], dst_ref=recv.at[rows(k), :], send_sem=send_sem.at[k], recv_sem=recv_sem.at[k],
-            device_id={'ep': peer(k, 1)}, device_id_type=MESH)
+        to = {1: (0, 1), 3: (side, 0), 5: (side, 1)}.get(k, dests[k])
+        return remote(send.at[rows(k), :], recv.at[rows(k), :], (send_sem.at[k], recv_sem.at[k]), to)
 
     def gate_copy(k):
-        return pltpu.make_async_remote_copy(
-            src_ref=sgate.at[k], dst_ref=rgate.at[k], send_sem=gsend_sem.at[k], recv_sem=grecv_sem.at[k],
-            device_id={'ep': peer(k, 1)}, device_id_type=MESH)
+        return remote(sgate.at[k], rgate.at[k], (gsend_sem.at[k], grecv_sem.at[k]), dests[k])
 
     def back_copy(k):
-        return pltpu.make_async_remote_copy(
-            src_ref=ysend.at[rows(k), :], dst_ref=yrecv.at[rows(k), :], send_sem=ysend_sem.at[k], recv_sem=yrecv_sem.at[k],
-            device_id={'ep': peer(k, -1)}, device_id_type=MESH)
+        return remote(ysend.at[rows(k), :], yrecv.at[rows(k), :], (ysend_sem.at[k], yrecv_sem.at[k]), homes[k])
+
+    raw_copy = remote(x_ref, raw, (raw_sem.at[0], raw_sem.at[1]), (side, 0))
+    rank_copy = remote(rank, rrank, (raw_sem.at[2], raw_sem.at[3]), (side, 0))
+
+    inputs[2].wait()
+    with scope('barrier'):
+        pl.semaphore_wait(barrier, groups - 1)
+    raw_copy.start()
 
     inputs[0].wait()
     inputs[1].wait()
@@ -74,23 +80,22 @@
     gates = gates_ref[...]
     dev = ids // local
     for k in range(groups):
-        chosen[k:k + 1, :] = jnp.max(jnp.where(dev == peer(k, 1), 1.0, 0.0), axis=0, keepdims=True)
+        chosen[k:k + 1, :] = jnp.max(jnp.where(dev == device(*dests[k]), 1.0, 0.0), axis=0, keepdims=True)
     flags = chosen[...]
     earlier = lax.broadcasted_iota(jnp.int32, (tok_dev, tok_dev), 0) < lax.broadcasted_iota(jnp.int32, (tok_dev, tok_dev), 1)
-    rank = jnp.dot(flags.astype(bf16), jnp.where(earlier, 1.0, 0.0).astype(bf16), preferred_element_type=f32)
-    rank = jnp.where(flags > 0.0, rank, -1.0).astype(jnp.int32)
-    row_id = lax.broadcasted_iota(jnp.int32, (lanes, tok_dev), 0)
-    loc_id = lax.broadcasted_iota(jnp.int32, (local, tok_dev), 0)
-    inputs[2].wait()
+    order = jnp.dot(flags.astype(bf16), jnp.where(earlier, 1.0, 0.0).astype(bf16), preferred_element_type=f32)
+    rank[...] = jnp.where(flags > 0.0, order, -1.0).astype(jnp.int32)
+    rank_copy.start()
     for e in range(local):
         for copy in weight_copies(e):
             copy.start()
 
-    for n, k in enumerate(others + [own]):
+    row_id = lax.broadcasted_iota(jnp.int32, (lanes, tok_dev), 0)
+    loc_id = lax.broadcasted_iota(jnp.int32, (local, tok_dev), 0)
+    for k in (7, 2, 4, 6, 0, 1, 3, 5):
         onehot = jnp.where(row_id == rank[k:k + 1, :], 1.0, 0.0).astype(bf16)
         pack[rows(k), :] = onehot[:cap, :]
-        packed = jnp.dot(onehot[:cap, :], x_ref[...], preferred_element_type=f32).astype(bf16)
-        first = peer(k, 1) * local
+        first = device(*dests[k]) * local
         gate = jnp.zeros((local, tok_dev), f32)
         for j in range(top_k):
             gate += jnp.where(ids[j:j + 1, :] - first == loc_id, gates[j:j + 1, :], 0.0)
@@ -101,16 +106,34 @@
         moved = lax.dot_general(parts, onehot, (((1,), (1,)), ((), ())), preferred_element_type=f32)
         moved = moved[:local] + moved[local:2 * local] + moved[2 * local:]
         if k == own:
-            recv[rows(k), :] = packed
             rgate[k] = moved
         else:
-            send[rows(k), :] = packed
             sgate[k] = moved
-            if n == 0:
-                with scope('barrier'):
-                    pl.semaphore_wait(barrier, groups - 1)
             gate_copy(k).start()
-            row_copy(k).start()
+        if k in direct + (7, own):
+            packed = jnp.dot(onehot[:cap, :], x_ref[...], preferred_element_type=f32).astype(bf16)
+            if k == own:
+                recv[rows(k), :] = packed
+            else:
+                send[rows(k), :] = packed
+                if k == 7:
+                    row_copy(k).start()
+    with scope('rawsend'):
+        raw_copy.wait_send()
+    for k in direct:
+        row_copy(k).start()
+    with scope('rawwait'):
+        rank_copy.wait_recv()
+        raw_copy.wait_recv()
+    with scope('relay'):
+        for k in (1, 3, 5, 0):
+            onehot = jnp.where(row_id[:cap, :] == rrank[k:k + 1, :], 1.0, 0.0).astype(bf16)
+            packed = jnp.dot(onehot, raw[...], preferred_element_type=f32).astype(bf16)
+            if k == 0:
+                recv[rows(k), :] = packed
+            else:
+                send[rows(k), :] = packed
+                row_copy(k).start()
 
     pair = 2 * cap
     half = ffn // 2
@@ -125,7 +148,8 @@
                     if k != own:
                         with scope('rwait%d' % k):
                             gate_copy(k).wait_recv()
-                            row_copy(k).wait_recv()
+                            if k > 0:
+                                row_copy(k).wait_recv()
                     gcol[(k % 2) * cap:(k % 2 + 1) * cap, :] = jnp.concatenate(
                         [rgate[k], jnp.zeros((lanes - local, lanes), f32)], axis=0).T[:cap, :]
         base = pl.multiple_of(b * pair, pair)
@@ -160,7 +184,7 @@
         for i in range(groups // 2):
             @pl.when(b == i)
             def _(i=i):
-                for k in (2 * i, 2 * i + 1):
+                for k in (2 * i + 1, 2 * i):
                     part = acc[(k % 2) * cap:(k % 2 + 1) * cap, :].astype(bf16)
                     if k == own:
                         yrecv[rows(k), :] = part
@@ -192,8 +216,10 @@
     with scope('sends'):
         for k in others:
             gate_copy(k).wait_send()
-            row_copy(k).wait_send()
+            if k > 0:
+                row_copy(k).wait_send()
             back_copy(k).wait_send()
+        rank_copy.wait_send()
 
 
 def solution(mesh):
@@ -224,6 +250,9 @@
                 pltpu.VMEM(w_up.shape, bf16),
                 pltpu.VMEM(w_down.shape, bf16),
                 pltpu.VMEM((groups, tok_dev), f32),
+                pltpu.VMEM((groups, tok_dev), jnp.int32),
+                pltpu.VMEM((groups, tok_dev), jnp.int32),
+                pltpu.VMEM(tokens.shape, bf16),
                 pltpu.VMEM((groups * cap, tok_dev), bf16),
                 pltpu.VMEM((groups * cap, d_model), bf16),
                 pltpu.VMEM((groups, local, lanes), f32),
@@ -237,6 +266,7 @@
                 pltpu.VMEM((tok_dev, d_model), f32),
                 pltpu.SemaphoreType.DMA((3,)),
                 pltpu.SemaphoreType.DMA((3, local)),
+                pltpu.SemaphoreType.DMA((4,)),
                 dma, dma, dma, dma, dma, dma,
             ],
             compiler_params=pltpu.CompilerParams(collective_id=0, has_side_effects=True, vmem_limit_bytes=54 * 1024 * 1024),

time: 59.6 us -> 56.4 us (0.946); the launches traced: 58.5 us -> 56.3 us
  Pallas kernels: 57.6 us -> 55.4 us
    pallas_call x1, Pallas kernels: 57.6 us -> 55.4 us  [device_step(): pl.pallas_call(functools.partial(moe_kernel, groups, cap), out_shape=pltp...]
where the time goes in v3:
time: 56.4 us; the launch traced here: 56.3 us
  Pallas kernels  55.4 us (98%)
  local copies, waits for them, and re-layouts  0.88 us (2%)
    pallas_call x1, Pallas kernels, device_step(): pl.pallas_call(functools.partial(moe_kernel, groups, cap), out_shape=pltp...  55.4 us

profile of v3, /device:TPU:112, one launch (start us, length us, event | category | flops | bytes accessed | tf_op | source)
XLA Modules:
  0.0 56.3 jit_solution(13906710850478359692)
XLA Ops:
  0.0 55.4 %shard_map.64 = bf16[256,1536]{1,0:T(8,128)(2,1)S(1)} custom-call(bf16[256,1536]{1,0:T(8,128)(2,1)} %x_hbm.1, s32[6,256]{1,0:T(8,128)} %bitcast.2, f32[6,256]{1,0:T(8,128)} %bitcast.3, bf16[8,1536,512]{2,1,0:T(8,128)(2,1)} %wg_hbm.1, bf16[8,1536,512]{2,1,0:T(8,128)(2,1)} %wu_hbm.1, bf16[8,512,1536]{2,1,0:T(8,128)(2,1)} %wd_hbm.1), custom_call_target="tpu_custom_call" | custom-call | tf_op jit(solution)/shard_map/pallas_call | solution.py:240
  55.4 0.9 %copy.8 = bf16[256,1536]{1,0:T(8,128)(2,1)} copy(bf16[256,1536]{1,0:T(8,128)(2,1)S(1)} %shard_map.64) | data formatting | bytes 1572864

commit v4 on v3

v4 whole, which is shorter than its diff:
```python
import contextlib
import functools

import jax
import jax.numpy as jnp
from jax import lax
from jax.experimental import pallas as pl
from jax.experimental.pallas import tpu as pltpu
from jax.sharding import PartitionSpec as P

MESH = pl.DeviceIdType.MESH
CORES = 2


def scope(name):
    return contextlib.nullcontext()


def moe_kernel(groups, cap, x_hbm, ids_hbm, gates_hbm, wg_hbm, wu_hbm, wd_hbm, out_ref,
               x_ref, ids_ref, gates_ref, wg, wu, wd, chosen, rank, rrank, raw, rpack, pack, send, sgate, recv, rgate,
               gcol, hid, acc, ysend, yrecv, total,
               in_sem, w_sem, raw_send, raw_recv, rank_sem, row_send, row_recv, gate_sem, back_send, back_recv):
    tok_dev, d_model = x_ref.shape
    local, _, ffn = wg.shape
    top_k = ids_ref.shape[0]
    lanes = sgate.shape[2]
    chips = groups // CORES
    batches = groups // 2
    pair = 2 * cap
    f32, bf16 = jnp.float32, jnp.bfloat16
    me = lax.axis_index('ep')
    chip, core = me // CORES, me % CORES
    side = 1 - 2 * core
    dests = [(side, 0), (side, 1), (-side, 0), (chips // 2, 0), (-side, 1), (chips // 2, 1), (0, 0), (0, 1)]
    homes = [(-side, 0), (side, 1), (side, 0), (chips // 2, 0), (-side, 1), (chips // 2, 1), (0, 0), (0, 1)]
    direct, near, own, partner = (2, 4), (1, 0, 3, 5), 6, 7
    relay_to = {1: (0, 1), 3: (side, 0), 5: (side, 1)}
    others = [k for k in range(groups) if k != own]

    def device(dx, dc):
        return lax.rem(chip + chips + dx, chips) * CORES + lax.rem(core + dc, CORES)

    def remote(src, dst, send_sem, recv_sem, to):
        return pltpu.make_async_remote_copy(
            src_ref=src, dst_ref=dst, send_sem=send_sem, recv_sem=recv_sem, device_id={'ep': device(*to)}, device_id_type=MESH)

    def rows(k, count=1):
        return pl.ds(k * cap, count * cap)

    barrier = pltpu.get_barrier_semaphore()
    for k in others:
        pl.semaphore_signal(barrier, inc=1, device_id={'ep': device(*dests[k])}, device_id_type=MESH)

    inputs = [pltpu.make_async_copy(src, dst, in_sem.at[i])
              for i, (src, dst) in enumerate(((ids_hbm, ids_ref), (gates_hbm, gates_ref), (x_hbm, x_ref)))]
    weights = [pltpu.make_async_copy(src, dst, w_sem.at[i])
               for i, (src, dst) in enumerate(((wg_hbm, wg), (wu_hbm, wu), (wd_hbm, wd)))]

    early = d_model // 2
    tail_cols = lanes
    halves = [slice(0, early), slice(early, d_model)]
    chunks = [(slice(0, early), 0, 0), (slice(early, d_model - tail_cols), 0, 1), (slice(d_model - tail_cols, d_model), 1, 1)]
    raw_copies = [remote(x_ref.at[:, cols], raw.at[:, cols], raw_send.at[i], raw_recv.at[j], (side, 0)) for cols, i, j in chunks]
    sent_cols = [slice(0, d_model - tail_cols), slice(d_model - tail_cols, d_model)]
    raw_sent = [remote(x_ref.at[:, cols], raw.at[:, cols], raw_send.at[i], raw_recv.at[0], (side, 0)) for i, cols in enumerate(sent_cols)]
    raw_came = [remote(x_ref.at[:, cols], raw.at[:, cols], raw_send.at[0], raw_recv.at[j], (side, 0)) for j, cols in enumerate(halves)]
    rank_copy = remote(rank, rrank, rank_sem.at[0], rank_sem.at[1], (side, 0))

    def row_copies(k):
        pieces = halves if k in relay_to else [slice(0, d_model)]
        return [remote(send.at[rows(k), cols], recv.at[rows(k), cols], row_send.at[0], row_recv.at[k // 2], relay_to.get(k, dests[k]))
                for cols in pieces]

    def gate_copy(k):
        return remote(sgate.at[k], rgate.at[k], gate_sem.at[0], gate_sem.at[1], dests[k])

    def back_copy(k):
        return remote(ysend.at[rows(k), :], yrecv.at[rows(k), :], back_send.at[0], back_recv.at[k // 2], homes[k])

    def wait_rows(i):
        first, count = {0: (1, 1), batches - 1: (partner, 1)}.get(i, (2 * i, 2))
        remote(send.at[rows(first, count), :], recv.at[rows(first, count), :], row_send.at[0], row_recv.at[i], (0, 1)).wait_recv()

    def wait_back(i):
        first, count = (partner, 1) if i == batches - 1 else (2 * i, 2)
        remote(ysend.at[rows(first, count), :], yrecv.at[rows(first, count), :], back_send.at[0], back_recv.at[i], (0, 1)).wait_recv()

    for copy in inputs:
        copy.start()
    inputs[2].wait()
    for copy in weights:
        copy.start()
    with scope('barrier'):
        pl.semaphore_wait(barrier, groups - 1)
    raw_copies[0].start()

    inputs[0].wait()
    inputs[1].wait()
    ids = ids_ref[...]
    gates = gates_ref[...]
    dev = ids // local
    for k in range(groups):
        chosen[k:k + 1, :] = jnp.max(jnp.where(dev == device(*dests[k]), 1.0, 0.0), axis=0, keepdims=True)
    flags = chosen[...]
    earlier = lax.broadcasted_iota(jnp.int32, (tok_dev, tok_dev), 0) < lax.broadcasted_iota(jnp.int32, (tok_dev, tok_dev), 1)
    order = jnp.dot(flags.astype(bf16), jnp.where(earlier, 1.0, 0.0).astype(bf16), preferred_element_type=f32)
    rank[...] = jnp.where(flags > 0.0, order, -1.0).astype(jnp.int32)
    rank_copy.start()

    row_id = lax.broadcasted_iota(jnp.int32, (lanes, tok_dev), 0)
    loc_id = lax.broadcasted_iota(jnp.int32, (local, tok_dev), 0)
    for k in (7, 2, 4, 6, 0, 1, 3, 5):
        onehot = jnp.where(row_id == rank[k:k + 1, :], 1.0, 0.0).astype(bf16)
        pack[rows(k), :] = onehot[:cap, :]
        first = device(*dests[k]) * local
        gate = jnp.zeros((local, tok_dev), f32)
        for j in range(top_k):
            gate += jnp.where(ids[j:j + 1, :] - first == loc_id, gates[j:j + 1, :], 0.0)
        high = gate.astype(bf16).astype(f32)
        mid = (gate - high).astype(bf16).astype(f32)
        low = gate - high - mid
        parts = jnp.concatenate([high, mid, low], axis=0).astype(bf16)
        moved = lax.dot_general(parts, onehot, (((1,), (1,)), ((), ())), preferred_element_type=f32)
        moved = moved[:local] + moved[local:2 * local] + moved[2 * local:]
        if k == own:
            rgate[groups] = moved
        else:
            sgate[k] = moved
    for k in others:
        gate_copy(k).start()
    for copy in raw_copies[1:]:
        copy.start()
    for k in (partner,) + direct + (own,):
        packed = jnp.dot(pack[rows(k), :], x_ref[...], preferred_element_type=f32).astype(bf16)
        if k == own:
            recv[rows(k), :] = packed
        else:
            send[rows(k), :] = packed
            if k == partner:
                for copy in row_copies(k):
                    copy.start()

    with scope('rankwait'):
        rank_copy.wait_recv()
    for i, k in enumerate(near):
        rpack[i * cap:(i + 1) * cap, :] = jnp.where(row_id[:cap, :] == rrank[k:k + 1, :], 1.0, 0.0).astype(bf16)

    def relay(i, h):
        k, cols = near[i], halves[h]
        packed = jnp.dot(rpack[i * cap:(i + 1) * cap, :], raw[:, cols], preferred_element_type=f32).astype(bf16)
        if k == 0:
            recv[rows(k), cols] = packed
        else:
            send[rows(k), cols] = packed

    with scope('raw0'):
        raw_came[0].wait_recv()
    with scope('relay0'):
        for i in range(4):
            relay(i, 0)
        row_copies(1)[0].start()
    with scope('gates'):
        remote(sgate.at[pl.ds(0, groups - 1)], rgate.at[pl.ds(0, groups - 1)], gate_sem.at[0], gate_sem.at[1], (0, 1)).wait_recv()
        for k in range(groups):
            mine = rgate[groups if k == own else k]
            gcol[k // 2, (k % 2) * cap:(k % 2 + 1) * cap, :] = jnp.concatenate(
                [mine, jnp.zeros((lanes - local, lanes), f32)], axis=0).T[:cap, :]
    with scope('rawsend'):
        raw_sent[0].wait_send()
        raw_sent[1].wait_send()
    for k in direct + (3,):
        row_copies(k)[0].start()
    with scope('raw1'):
        raw_came[1].wait_recv()
    with scope('relay1'):
        for i, k in enumerate(near):
            relay(i, 1)
            if k == 5:
                row_copies(k)[0].start()
            if k > 0:
                row_copies(k)[1].start()

    half = ffn // 2
    third = d_model // 3
    lane_id = lax.broadcasted_iota(jnp.int32, (pair, lanes), 1)

    def hidden(e, base):
        for n in range(2):
            cols = slice(n * half, (n + 1) * half)
            g = jnp.dot(recv[pl.ds(base, pair), :], wg[e, :, cols], preferred_element_type=f32)
            u = jnp.dot(recv[pl.ds(base, pair), :], wu[e, :, cols], preferred_element_type=f32)
            hid[e % 2, :, cols] = (jax.nn.silu(g) * u).astype(bf16)

    def down(e, b, base):
        gate = jnp.sum(jnp.where(lane_id == e, gcol[b], 0.0), axis=1, keepdims=True)
        for n in range(3):
            cols = slice(n * third, (n + 1) * third)
            y = jnp.dot(hid[e % 2], wd[e, :, cols], preferred_element_type=f32).astype(bf16).astype(f32)
            y = jnp.where(gate > 0.0, gate * y, 0.0)
            if e == 0:
                acc[:, cols] = y
            elif e < local - 1:
                acc[:, cols] += y
            else:
                ysend[pl.ds(base, pair), cols] = (acc[:, cols] + y).astype(bf16)

    def batch(b, carry):
        base = pl.multiple_of(b * pair, pair)
        for i in range(batches):
            @pl.when(b == i)
            def _(i=i):
                with scope('rwait%d' % i):
                    wait_rows(i)
        with scope('steps'):
            hidden(0, base)
            for e in range(1, local):
                hidden(e, base)
                down(e - 1, b, base)
            down(local - 1, b, base)
        for i in range(batches):
            @pl.when(b == i)
            def _(i=i):
                for k in (2 * i + 1, 2 * i):
                    if k == own:
                        yrecv[rows(k), :] = ysend[rows(k), :]
                    else:
                        back_copy(k).start()
        return carry

    with scope('weights'):
        for copy in weights:
            copy.wait()
    lax.fori_loop(0, batches, batch, 0)

    ends = list(range(batches))
    ends[-2:] = ends[:-3:-1]
    for n, i in enumerate(ends):
        with scope('ywait%d' % i):
            wait_back(i)
        span = slice(i * pair, (i + 1) * pair)
        part = lax.dot_general(pack[span, :], yrecv[span, :], (((0,), (0,)), ((), ())), preferred_element_type=f32)
        if n == 0:
            total[...] = x_ref[...].astype(f32) + part
        elif n < batches - 1:
            total[...] += part
        else:
            out_ref[...] = (total[...] + part).astype(bf16)
    with scope('sends'):
        rank_copy.wait_send()
        remote(send.at[pl.ds(0, 6 * cap), :], recv.at[pl.ds(0, 6 * cap), :], row_send.at[0], row_recv.at[0], (0, 1)).wait_send()
        remote(sgate.at[pl.ds(0, groups - 1)], rgate.at[pl.ds(0, groups - 1)], gate_sem.at[0], gate_sem.at[1], (0, 1)).wait_send()
        remote(ysend.at[rows(0, groups - 1), :], yrecv.at[rows(0, groups - 1), :], back_send.at[0], back_recv.at[0], (0, 1)).wait_send()


def solution(mesh):
    groups = mesh.shape['ep']
    row_spec = P(('dp', 'ep'))
    expert_spec = P('ep')

    def device_step(tokens, expert_ids, gate_vals, w_gate, w_up, w_down):
        tok_dev, top_k = expert_ids.shape
        d_model = tokens.shape[1]
        local, _, ffn = w_gate.shape
        cap = tok_dev * (top_k // 2) // groups
        lanes = 128
        f32, bf16 = jnp.float32, jnp.bfloat16
        slots = groups * cap
        dma = pltpu.SemaphoreType.DMA
        return pl.pallas_call(
            functools.partial(moe_kernel, groups, cap),
            out_shape=pltpu.VMEM((tok_dev, d_model), bf16),
            in_specs=[pl.BlockSpec(memory_space=pl.ANY)] * 6,
            out_specs=pl.BlockSpec(memory_space=pltpu.VMEM),
            scratch_shapes=[
                pltpu.VMEM(tokens.shape, bf16),
                pltpu.VMEM((top_k, tok_dev), jnp.int32),
                pltpu.VMEM((top_k, tok_dev), f32),
                pltpu.VMEM(w_gate.shape, bf16),
                pltpu.VMEM(w_up.shape, bf16),
                pltpu.VMEM(w_down.shape, bf16),
                pltpu.VMEM((groups, tok_dev), f32),
                pltpu.VMEM((groups, tok_dev), jnp.int32),
                pltpu.VMEM((groups, tok_dev), jnp.int32),
                pltpu.VMEM(tokens.shape, bf16),
                pltpu.VMEM((slots // 2, tok_dev), bf16),
                pltpu.VMEM((slots, tok_dev), bf16),
                pltpu.VMEM((slots, d_model), bf16),
                pltpu.VMEM((groups, local, lanes), f32),
                pltpu.VMEM((slots, d_model), bf16),
                pltpu.VMEM((groups + 1, local, lanes), f32),
                pltpu.VMEM((groups // 2, 2 * cap, lanes), f32),
                pltpu.VMEM((2, 2 * cap, ffn), bf16),
                pltpu.VMEM((2 * cap, d_model), f32),
                pltpu.VMEM((slots, d_model), bf16),
                pltpu.VMEM((slots, d_model), bf16),
                pltpu.VMEM((tok_dev, d_model), f32),
                dma((3,)), dma((3,)), dma((2,)), dma((2,)), dma((2,)),
                dma((1,)), dma((groups // 2,)), dma((2,)), dma((1,)), dma((groups // 2,)),
            ],
            compiler_params=pltpu.CompilerParams(collective_id=0, has_side_effects=True, vmem_limit_bytes=56 * 1024 * 1024),
        )(tokens, expert_ids.T, gate_vals.T, w_gate, w_up, w_down)

    return jax.shard_map(device_step, mesh=mesh, in_specs=(row_spec, row_spec, row_spec, expert_spec, expert_spec, expert_spec), out_specs=row_spec, check_vma=False)
```

time: 56.4 us -> 55.4 us (0.982)
  Pallas kernels: 55.4 us -> 54.4 us
    pallas_call x1, Pallas kernels: 55.4 us -> 54.4 us  [device_step(): pl.pallas_call(functools.partial(moe_kernel, groups, cap), out_shape=pltp...]
where the time goes in v4:
time: 55.4 us; the launch traced here: 55.3 us
  Pallas kernels  54.4 us (98%)
  local copies, waits for them, and re-layouts  0.88 us (2%)
    pallas_call x1, Pallas kernels, device_step(): pl.pallas_call(functools.partial(moe_kernel, groups, cap), out_shape=pltp...  54.4 us

profile of v4, /device:TPU:112, one launch (start us, length us, event | category | flops | bytes accessed | tf_op | source)
XLA Modules:
  0.0 55.3 jit_solution(7098324420758709536)
XLA Ops:
  0.0 54.4 %shard_map.64 = bf16[256,1536]{1,0:T(8,128)(2,1)S(1)} custom-call(bf16[256,1536]{1,0:T(8,128)(2,1)} %x_hbm.1, s32[6,256]{1,0:T(8,128)} %bitcast.2, f32[6,256]{1,0:T(8,128)} %bitcast.3, bf16[8,1536,512]{2,1,0:T(8,128)(2,1)} %wg_hbm.1, bf16[8,1536,512]{2,1,0:T(8,128)(2,1)} %wu_hbm.1, bf16[8,512,1536]{2,1,0:T(8,128)(2,1)} %wd_hbm.1), custom_call_target="tpu_custom_call" | custom-call | tf_op jit(solution)/shard_map/pallas_call | solution.py:269
  54.4 0.9 %copy.8 = bf16[256,1536]{1,0:T(8,128)(2,1)} copy(bf16[256,1536]{1,0:T(8,128)(2,1)S(1)} %shard_map.64) | data formatting | bytes 1572864

commit v5 on v4

--- a/solution.py
+++ b/solution.py
@@ -17,9 +17,9 @@
 
 
 def moe_kernel(groups, cap, x_hbm, ids_hbm, gates_hbm, wg_hbm, wu_hbm, wd_hbm, out_ref,
-               x_ref, ids_ref, gates_ref, wg, wu, wd, chosen, rank, rrank, raw, rpack, pack, send, sgate, recv, rgate,
+               x_ref, ids_ref, gates_ref, wg, wu, wd, chosen, rank, nrank, rrank, raw, rpack, pack, send, sgate, recv, rgate,
                gcol, hid, acc, ysend, yrecv, total,
-               in_sem, w_sem, raw_send, raw_recv, rank_sem, row_send, row_recv, gate_sem, back_send, back_recv):
+               in_sem, w_sem, raw_send, raw_recv, rank_sem, row_send, row_recv, gate_sem, back_send, back_recv, known):
     tok_dev, d_model = x_ref.shape
     local, _, ffn = wg.shape
     top_k = ids_ref.shape[0]
@@ -47,9 +47,12 @@
     def rows(k, count=1):
         return pl.ds(k * cap, count * cap)
 
+    def tell(sem, to):
+        pl.semaphore_signal(sem, inc=1, device_id={'ep': device(*to)}, device_id_type=MESH)
+
     barrier = pltpu.get_barrier_semaphore()
-    for k in others:
-        pl.semaphore_signal(barrier, inc=1, device_id={'ep': device(*dests[k])}, device_id_type=MESH)
+    tell(barrier, (-side, 0))
+    tell(barrier, (0, 1))
 
     inputs = [pltpu.make_async_copy(src, dst, in_sem.at[i])
               for i, (src, dst) in enumerate(((ids_hbm, ids_ref), (gates_hbm, gates_ref), (x_hbm, x_ref)))]
@@ -57,14 +60,9 @@
                for i, (src, dst) in enumerate(((wg_hbm, wg), (wu_hbm, wu), (wd_hbm, wd)))]
 
     early = d_model // 2
-    tail_cols = lanes
     halves = [slice(0, early), slice(early, d_model)]
-    chunks = [(slice(0, early), 0, 0), (slice(early, d_model - tail_cols), 0, 1), (slice(d_model - tail_cols, d_model), 1, 1)]
-    raw_copies = [remote(x_ref.at[:, cols], raw.at[:, cols], raw_send.at[i], raw_recv.at[j], (side, 0)) for cols, i, j in chunks]
-    sent_cols = [slice(0, d_model - tail_cols), slice(d_model - tail_cols, d_model)]
-    raw_sent = [remote(x_ref.at[:, cols], raw.at[:, cols], raw_send.at[i], raw_recv.at[0], (side, 0)) for i, cols in enumerate(sent_cols)]
-    raw_came = [remote(x_ref.at[:, cols], raw.at[:, cols], raw_send.at[0], raw_recv.at[j], (side, 0)) for j, cols in enumerate(halves)]
-    rank_copy = remote(rank, rrank, rank_sem.at[0], rank_sem.at[1], (side, 0))
+    raw_copies = [remote(x_ref.at[:, cols], raw.at[:, cols], raw_send.at[h], raw_recv.at[h], (side, 0)) for h, cols in enumerate(halves)]
+    rank_copy = remote(nrank, rrank, rank_sem.at[0], rank_sem.at[1], (side, 0))
 
     def row_copies(k):
         pieces = halves if k in relay_to else [slice(0, d_model)]
@@ -74,16 +72,21 @@
     def gate_copy(k):
         return remote(sgate.at[k], rgate.at[k], gate_sem.at[0], gate_sem.at[1], dests[k])
 
-    def back_copy(k):
-        return remote(ysend.at[rows(k), :], yrecv.at[rows(k), :], back_send.at[0], back_recv.at[k // 2], homes[k])
+    final = batches - 2
+
+    def back_copies(k):
+        pieces = halves if k // 2 == final else [slice(0, d_model)]
+        return [remote(ysend.at[rows(k), cols], yrecv.at[rows(k), cols], back_send.at[0], back_recv.at[batches if h else k // 2], homes[k])
+                for h, cols in enumerate(pieces)]
 
     def wait_rows(i):
         first, count = {0: (1, 1), batches - 1: (partner, 1)}.get(i, (2 * i, 2))
         remote(send.at[rows(first, count), :], recv.at[rows(first, count), :], row_send.at[0], row_recv.at[i], (0, 1)).wait_recv()
 
-    def wait_back(i):
+    def wait_back(i, cols=slice(0, d_model), sem=None):
         first, count = (partner, 1) if i == batches - 1 else (2 * i, 2)
-        remote(ysend.at[rows(first, count), :], yrecv.at[rows(first, count), :], back_send.at[0], back_recv.at[i], (0, 1)).wait_recv()
+        remote(ysend.at[rows(first, count), cols], yrecv.at[rows(first, count), cols], back_send.at[0],
+               back_recv.at[i if sem is None else sem], (0, 1)).wait_recv()
 
     for copy in inputs:
         copy.start()
@@ -91,7 +94,8 @@
     for copy in weights:
         copy.start()
     with scope('barrier'):
-        pl.semaphore_wait(barrier, groups - 1)
+        pl.semaphore_wait(barrier, 2)
+    tell(known.at[0], (side, 0))
     raw_copies[0].start()
 
     inputs[0].wait()
@@ -105,7 +109,12 @@
     earlier = lax.broadcasted_iota(jnp.int32, (tok_dev, tok_dev), 0) < lax.broadcasted_iota(jnp.int32, (tok_dev, tok_dev), 1)
     order = jnp.dot(flags.astype(bf16), jnp.where(earlier, 1.0, 0.0).astype(bf16), preferred_element_type=f32)
     rank[...] = jnp.where(flags > 0.0, order, -1.0).astype(jnp.int32)
+    for i, k in enumerate(near):
+        nrank[i:i + 1, :] = rank[k:k + 1, :]
     rank_copy.start()
+    with scope('known0'):
+        pl.semaphore_wait(known.at[0], 1)
+    tell(known.at[1], (-side, 0))
 
     row_id = lax.broadcasted_iota(jnp.int32, (lanes, tok_dev), 0)
     loc_id = lax.broadcasted_iota(jnp.int32, (local, tok_dev), 0)
@@ -126,10 +135,14 @@
             rgate[groups] = moved
         else:
             sgate[k] = moved
+    with scope('known1'):
+        pl.semaphore_wait(known.at[1], 1)
+    tell(known.at[2], (0, 1))
+    with scope('known2'):
+        pl.semaphore_wait(known.at[2], 1)
     for k in others:
         gate_copy(k).start()
-    for copy in raw_copies[1:]:
-        copy.start()
+    raw_copies[1].start()
     for k in (partner,) + direct + (own,):
         packed = jnp.dot(pack[rows(k), :], x_ref[...], preferred_element_type=f32).astype(bf16)
         if k == own:
@@ -143,7 +156,7 @@
     with scope('rankwait'):
         rank_copy.wait_recv()
     for i, k in enumerate(near):
-        rpack[i * cap:(i + 1) * cap, :] = jnp.where(row_id[:cap, :] == rrank[k:k + 1, :], 1.0, 0.0).astype(bf16)
+        rpack[i * cap:(i + 1) * cap, :] = jnp.where(row_id[:cap, :] == rrank[i:i + 1, :], 1.0, 0.0).astype(bf16)
 
     def relay(i, h):
         k, cols = near[i], halves[h]
@@ -154,11 +167,12 @@
             send[rows(k), cols] = packed
 
     with scope('raw0'):
-        raw_came[0].wait_recv()
+        raw_copies[0].wait_recv()
     with scope('relay0'):
         for i in range(4):
             relay(i, 0)
-        row_copies(1)[0].start()
+        for k in (1, 3):
+            row_copies(k)[0].start()
     with scope('gates'):
         remote(sgate.at[pl.ds(0, groups - 1)], rgate.at[pl.ds(0, groups - 1)], gate_sem.at[0], gate_sem.at[1], (0, 1)).wait_recv()
         for k in range(groups):
@@ -166,12 +180,12 @@
             gcol[k // 2, (k % 2) * cap:(k % 2 + 1) * cap, :] = jnp.concatenate(
                 [mine, jnp.zeros((lanes - local, lanes), f32)], axis=0).T[:cap, :]
     with scope('rawsend'):
-        raw_sent[0].wait_send()
-        raw_sent[1].wait_send()
-    for k in direct + (3,):
+        raw_copies[0].wait_send()
+        raw_copies[1].wait_send()
+    for k in direct:
         row_copies(k)[0].start()
     with scope('raw1'):
-        raw_came[1].wait_recv()
+        raw_copies[1].wait_recv()
     with scope('relay1'):
         for i, k in enumerate(near):
             relay(i, 1)
@@ -220,11 +234,11 @@
         for i in range(batches):
             @pl.when(b == i)
             def _(i=i):
-                for k in (2 * i + 1, 2 * i):
-                    if k == own:
-                        yrecv[rows(k), :] = ysend[rows(k), :]
-                    else:
-                        back_copy(k).start()
+                if i == own // 2:
+                    yrecv[rows(own), :] = ysend[rows(own), :]
+                for copies in zip(*[back_copies(k) for k in (2 * i + 1, 2 * i) if k != own]):
+                    for copy in copies:
+                        copy.start()
         return carry
 
     with scope('weights'):
@@ -232,19 +246,19 @@
             copy.wait()
     lax.fori_loop(0, batches, batch, 0)
 
-    ends = list(range(batches))
-    ends[-2:] = ends[:-3:-1]
-    for n, i in enumerate(ends):
+    def combine(i, cols):
+        span = slice(i * pair, (i + 1) * pair)
+        return lax.dot_general(pack[span, :], yrecv[span, cols], (((0,), (0,)), ((), ())), preferred_element_type=f32)
+
+    everything = slice(0, d_model)
+    for n, i in enumerate((0, batches - 1, 1)):
         with scope('ywait%d' % i):
             wait_back(i)
-        span = slice(i * pair, (i + 1) * pair)
-        part = lax.dot_general(pack[span, :], yrecv[span, :], (((0,), (0,)), ((), ())), preferred_element_type=f32)
-        if n == 0:
-            total[...] = x_ref[...].astype(f32) + part
-        elif n < batches - 1:
-            total[...] += part
-        else:
-            out_ref[...] = (total[...] + part).astype(bf16)
+        total[...] = (x_ref[...].astype(f32) if n == 0 else total[...]) + combine(i, everything)
+    for h, cols in enumerate(halves):
+        with scope('yfinal%d' % h):
+            wait_back(final, cols, batches if h else final)
+        out_ref[:, cols] = (total[:, cols] + combine(final, cols)).astype(bf16)
     with scope('sends'):
         rank_copy.wait_send()
         remote(send.at[pl.ds(0, 6 * cap), :], recv.at[pl.ds(0, 6 * cap), :], row_send.at[0], row_recv.at[0], (0, 1)).wait_send()
@@ -280,7 +294,8 @@
                 pltpu.VMEM(w_down.shape, bf16),
                 pltpu.VMEM((groups, tok_dev), f32),
                 pltpu.VMEM((groups, tok_dev), jnp.int32),
-                pltpu.VMEM((groups, tok_dev), jnp.int32),
+                pltpu.VMEM((groups // 2, tok_dev), jnp.int32),
+                pltpu.VMEM((groups // 2, tok_dev), jnp.int32),
                 pltpu.VMEM(tokens.shape, bf16),
                 pltpu.VMEM((slots // 2, tok_dev), bf16),
                 pltpu.VMEM((slots, tok_dev), bf16),
@@ -295,7 +310,7 @@
                 pltpu.VMEM((slots, d_model), bf16),
                 pltpu.VMEM((tok_dev, d_model), f32),
                 dma((3,)), dma((3,)), dma((2,)), dma((2,)), dma((2,)),
-                dma((1,)), dma((groups // 2,)), dma((2,)), dma((1,)), dma((groups // 2,)),
+                dma((1,)), dma((groups // 2,)), dma((2,)), dma((1,)), dma((groups // 2 + 1,)), pltpu.SemaphoreType.REGULAR((3,)),
             ],
             compiler_params=pltpu.CompilerParams(collective_id=0, has_side_effects=True, vmem_limit_bytes=56 * 1024 * 1024),
         )(tokens, expert_ids.T, gate_vals.T, w_gate, w_up, w_down)

time: 55.4 us -> 54.8 us (0.989)
  no operation moved by 1% of the time
where the time goes in v5:
time: 54.8 us; the launch traced here: 54.7 us
  Pallas kernels  53.9 us (98%)
  local copies, waits for them, and re-layouts  0.88 us (2%)
    pallas_call x1, Pallas kernels, device_step(): pl.pallas_call(functools.partial(moe_kernel, groups, cap), out_shape=pltp...  53.9 us

profile of v5, /device:TPU:112, one launch (start us, length us, event | category | flops | bytes accessed | tf_op | source)
XLA Modules:
  0.0 54.7 jit_solution(18131966199700972525)
XLA Ops:
  0.0 53.9 %shard_map.64 = bf16[256,1536]{1,0:T(8,128)(2,1)S(1)} custom-call(bf16[256,1536]{1,0:T(8,128)(2,1)} %x_hbm.1, s32[6,256]{1,0:T(8,128)} %bitcast.2, f32[6,256]{1,0:T(8,128)} %bitcast.3, bf16[8,1536,512]{2,1,0:T(8,128)(2,1)} %wg_hbm.1, bf16[8,1536,512]{2,1,0:T(8,128)(2,1)} %wu_hbm.1, bf16[8,512,1536]{2,1,0:T(8,128)(2,1)} %wd_hbm.1), custom_call_target="tpu_custom_call" | custom-call | tf_op jit(solution)/shard_map/pallas_call | solution.py:283
  53.9 0.9 %copy.8 = bf16[256,1536]{1,0:T(8,128)(2,1)} copy(bf16[256,1536]{1,0:T(8,128)(2,1)S(1)} %shard_map.64) | data formatting | bytes 1572864

commit v6 on v5

--- a/solution.py
+++ b/solution.py
@@ -118,6 +118,7 @@
 
     row_id = lax.broadcasted_iota(jnp.int32, (lanes, tok_dev), 0)
     loc_id = lax.broadcasted_iota(jnp.int32, (local, tok_dev), 0)
+    expert = lax.broadcasted_iota(jnp.int32, (local, lanes), 0).astype(f32)
     for k in (7, 2, 4, 6, 0, 1, 3, 5):
         onehot = jnp.where(row_id == rank[k:k + 1, :], 1.0, 0.0).astype(bf16)
         pack[rows(k), :] = onehot[:cap, :]
@@ -131,6 +132,10 @@
         parts = jnp.concatenate([high, mid, low], axis=0).astype(bf16)
         moved = lax.dot_general(parts, onehot, (((1,), (1,)), ((), ())), preferred_element_type=f32)
         moved = moved[:local] + moved[local:2 * local] + moved[2 * local:]
+        low_id = jnp.min(jnp.where(moved > 0.0, expert, float(local)), axis=0, keepdims=True)
+        high_id = jnp.max(jnp.where(moved > 0.0, expert, -1.0), axis=0, keepdims=True)
+        moved = jnp.concatenate([jnp.sum(jnp.where(expert == low_id, moved, 0.0), axis=0, keepdims=True),
+                                 jnp.sum(jnp.where(expert == high_id, moved, 0.0), axis=0, keepdims=True), low_id, high_id], axis=0)
         if k == own:
             rgate[groups] = moved
         else:
@@ -176,7 +181,8 @@
     with scope('gates'):
         remote(sgate.at[pl.ds(0, groups - 1)], rgate.at[pl.ds(0, groups - 1)], gate_sem.at[0], gate_sem.at[1], (0, 1)).wait_recv()
         for k in range(groups):
-            mine = rgate[groups if k == own else k]
+            two = rgate[groups if k == own else k]
+            mine = jnp.where(expert == two[2:3], two[0:1], jnp.where(expert == two[3:4], two[1:2], 0.0))
             gcol[k // 2, (k % 2) * cap:(k % 2 + 1) * cap, :] = jnp.concatenate(
                 [mine, jnp.zeros((lanes - local, lanes), f32)], axis=0).T[:cap, :]
     with scope('rawsend'):
@@ -300,9 +306,9 @@
                 pltpu.VMEM((slots // 2, tok_dev), bf16),
                 pltpu.VMEM((slots, tok_dev), bf16),
                 pltpu.VMEM((slots, d_model), bf16),
-                pltpu.VMEM((groups, local, lanes), f32),
+                pltpu.VMEM((groups, 4, lanes), f32),
                 pltpu.VMEM((slots, d_model), bf16),
-                pltpu.VMEM((groups + 1, local, lanes), f32),
+                pltpu.VMEM((groups + 1, 4, lanes), f32),
                 pltpu.VMEM((groups // 2, 2 * cap, lanes), f32),
                 pltpu.VMEM((2, 2 * cap, ffn), bf16),
                 pltpu.VMEM((2 * cap, d_model), f32),

time: 54.8 us -> 54.6 us (level)
  no operation moved by 1% of the time
where the time goes in v6:
time: 54.6 us; the launch traced here: 54.5 us
  Pallas kernels  53.6 us (98%)
  local copies, waits for them, and re-layouts  0.88 us (2%)
    pallas_call x1, Pallas kernels, device_step(): pl.pallas_call(functools.partial(moe_kernel, groups, cap), out_shape=pltp...  53.6 us

profile of v6, /device:TPU:112, one launch (start us, length us, event | category | flops | bytes accessed | tf_op | source)
XLA Modules:
  0.0 54.5 jit_solution(17538422779817279078)
XLA Ops:
  0.0 53.6 %shard_map.64 = bf16[256,1536]{1,0:T(8,128)(2,1)S(1)} custom-call(bf16[256,1536]{1,0:T(8,128)(2,1)} %x_hbm.1, s32[6,256]{1,0:T(8,128)} %bitcast.2, f32[6,256]{1,0:T(8,128)} %bitcast.3, bf16[8,1536,512]{2,1,0:T(8,128)(2,1)} %wg_hbm.1, bf16[8,1536,512]{2,1,0:T(8,128)(2,1)} %wu_hbm.1, bf16[8,512,1536]{2,1,0:T(8,128)(2,1)} %wd_hbm.1), custom_call_target="tpu_custom_call" | custom-call | tf_op jit(solution)/shard_map/pallas_call | solution.py:289
  53.7 0.9 %copy.8 = bf16[256,1536]{1,0:T(8,128)(2,1)} copy(bf16[256,1536]{1,0:T(8,128)(2,1)S(1)} %shard_map.64) | data formatting | bytes 1572864

commit v7 on v6

--- a/solution.py
+++ b/solution.py
@@ -59,7 +59,7 @@
     weights = [pltpu.make_async_copy(src, dst, w_sem.at[i])
                for i, (src, dst) in enumerate(((wg_hbm, wg), (wu_hbm, wu), (wd_hbm, wd)))]
 
-    early = d_model // 2
+    early = d_model * 2 // 3
     halves = [slice(0, early), slice(early, d_model)]
     raw_copies = [remote(x_ref.at[:, cols], raw.at[:, cols], raw_send.at[h], raw_recv.at[h], (side, 0)) for h, cols in enumerate(halves)]
     rank_copy = remote(nrank, rrank, rank_sem.at[0], rank_sem.at[1], (side, 0))
@@ -126,7 +126,7 @@
         gate = jnp.zeros((local, tok_dev), f32)
         for j in range(top_k):
             gate += jnp.where(ids[j:j + 1, :] - first == loc_id, gates[j:j + 1, :], 0.0)
-        high = gate.astype(bf16).astype(f32)
+        high = jnp.minimum(gate, float(jnp.finfo(bf16).max)).astype(bf16).astype(f32)
         mid = (gate - high).astype(bf16).astype(f32)
         low = gate - high - mid
         parts = jnp.concatenate([high, mid, low], axis=0).astype(bf16)

time: 54.6 us -> 54.6 us (level)
  no operation moved by 1% of the time
where the time goes in v7:
time: 54.6 us; the launch traced here: 54.5 us
  Pallas kernels  53.6 us (98%)
  local copies, waits for them, and re-layouts  0.88 us (2%)
    pallas_call x1, Pallas kernels, device_step(): pl.pallas_call(functools.partial(moe_kernel, groups, cap), out_shape=pltp...  53.6 us

profile of v7, /device:TPU:112, one launch (start us, length us, event | category | flops | bytes accessed | tf_op | source)
XLA Modules:
  0.0 54.5 jit_solution(12338355603036653148)
XLA Ops:
  0.0 53.6 %shard_map.64 = bf16[256,1536]{1,0:T(8,128)(2,1)S(1)} custom-call(bf16[256,1536]{1,0:T(8,128)(2,1)} %x_hbm.1, s32[6,256]{1,0:T(8,128)} %bitcast.2, f32[6,256]{1,0:T(8,128)} %bitcast.3, bf16[8,1536,512]{2,1,0:T(8,128)(2,1)} %wg_hbm.1, bf16[8,1536,512]{2,1,0:T(8,128)(2,1)} %wu_hbm.1, bf16[8,512,1536]{2,1,0:T(8,128)(2,1)} %wd_hbm.1), custom_call_target="tpu_custom_call" | custom-call | tf_op jit(solution)/shard_map/pallas_call | solution.py:289
  53.6 0.9 %copy.8 = bf16[256,1536]{1,0:T(8,128)(2,1)} copy(bf16[256,1536]{1,0:T(8,128)(2,1)S(1)} %shard_map.64) | data formatting | bytes 1572864

commit v8 on v7

--- a/solution.py
+++ b/solution.py
@@ -61,7 +61,7 @@
 
     early = d_model * 2 // 3
     halves = [slice(0, early), slice(early, d_model)]
-    raw_copies = [remote(x_ref.at[:, cols], raw.at[:, cols], raw_send.at[h], raw_recv.at[h], (side, 0)) for h, cols in enumerate(halves)]
+    raw_copies = [remote(x_ref.at[:, cols], raw.at[:, cols], raw_send.at[0], raw_recv.at[h], (side, 0)) for h, cols in enumerate(halves)]
     rank_copy = remote(nrank, rrank, rank_sem.at[0], rank_sem.at[1], (side, 0))
 
     def row_copies(k):
@@ -76,17 +76,15 @@
 
     def back_copies(k):
         pieces = halves if k // 2 == final else [slice(0, d_model)]
-        return [remote(ysend.at[rows(k), cols], yrecv.at[rows(k), cols], back_send.at[0], back_recv.at[batches if h else k // 2], homes[k])
+        return [remote(ysend.at[rows(k), cols], yrecv.at[rows(k), cols], back_send.at[0], back_recv.at[0 if k // 2 != final else 1 + h], homes[k])
                 for h, cols in enumerate(pieces)]
 
     def wait_rows(i):
         first, count = {0: (1, 1), batches - 1: (partner, 1)}.get(i, (2 * i, 2))
         remote(send.at[rows(first, count), :], recv.at[rows(first, count), :], row_send.at[0], row_recv.at[i], (0, 1)).wait_recv()
 
-    def wait_back(i, cols=slice(0, d_model), sem=None):
-        first, count = (partner, 1) if i == batches - 1 else (2 * i, 2)
-        remote(ysend.at[rows(first, count), cols], yrecv.at[rows(first, count), cols], back_send.at[0],
-               back_recv.at[i if sem is None else sem], (0, 1)).wait_recv()
+    def wait_back(first, count, cols, sem):
+        remote(ysend.at[rows(first, count), cols], yrecv.at[rows(first, count), cols], back_send.at[0], back_recv.at[sem], (0, 1)).wait_recv()
 
     for copy in inputs:
         copy.start()
@@ -186,8 +184,7 @@
             gcol[k // 2, (k % 2) * cap:(k % 2 + 1) * cap, :] = jnp.concatenate(
                 [mine, jnp.zeros((lanes - local, lanes), f32)], axis=0).T[:cap, :]
     with scope('rawsend'):
-        raw_copies[0].wait_send()
-        raw_copies[1].wait_send()
+        remote(x_ref, raw, raw_send.at[0], raw_recv.at[0], (side, 0)).wait_send()
     for k in direct:
         row_copies(k)[0].start()
     with scope('raw1'):
@@ -257,13 +254,12 @@
         return lax.dot_general(pack[span, :], yrecv[span, cols], (((0,), (0,)), ((), ())), preferred_element_type=f32)
 
     everything = slice(0, d_model)
-    for n, i in enumerate((0, batches - 1, 1)):
-        with scope('ywait%d' % i):
-            wait_back(i)
-        total[...] = (x_ref[...].astype(f32) if n == 0 else total[...]) + combine(i, everything)
+    wait_back(0, groups - 3, everything, 0)
+    total[...] = x_ref[...].astype(f32) + combine(0, everything)
+    for i in (1, batches - 1):
+        total[...] += combine(i, everything)
     for h, cols in enumerate(halves):
-        with scope('yfinal%d' % h):
-            wait_back(final, cols, batches if h else final)
+        wait_back(2 * final, 2, cols, 1 + h)
         out_ref[:, cols] = (total[:, cols] + combine(final, cols)).astype(bf16)
     with scope('sends'):
         rank_copy.wait_send()
@@ -315,8 +311,8 @@
                 pltpu.VMEM((slots, d_model), bf16),
                 pltpu.VMEM((slots, d_model), bf16),
                 pltpu.VMEM((tok_dev, d_model), f32),
-                dma((3,)), dma((3,)), dma((2,)), dma((2,)), dma((2,)),
-                dma((1,)), dma((groups // 2,)), dma((2,)), dma((1,)), dma((groups // 2 + 1,)), pltpu.SemaphoreType.REGULAR((3,)),
+                dma((3,)), dma((3,)), dma((1,)), dma((2,)), dma((2,)),
+                dma((1,)), dma((groups // 2,)), dma((2,)), dma((1,)), dma((3,)), pltpu.SemaphoreType.REGULAR((3,)),
             ],
             compiler_params=pltpu.CompilerParams(collective_id=0, has_side_effects=True, vmem_limit_bytes=56 * 1024 * 1024),
         )(tokens, expert_ids.T, gate_vals.T, w_gate, w_up, w_down)

time: 54.6 us -> 54.6 us (level)
  no operation moved by 1% of the time
where the time goes in v8:
time: 54.6 us; the launch traced here: 54.5 us
  Pallas kernels  53.6 us (98%)
  local copies, waits for them, and re-layouts  0.88 us (2%)
    pallas_call x1, Pallas kernels, device_step(): pl.pallas_call(functools.partial(moe_kernel, groups, cap), out_shape=pltp...  53.6 us

profile of v8, /device:TPU:112, one launch (start us, length us, event | category | flops | bytes accessed | tf_op | source)
XLA Modules:
  0.0 54.5 jit_solution(8285315445753256049)
XLA Ops:
  0.0 53.6 %shard_map.64 = bf16[256,1536]{1,0:T(8,128)(2,1)S(1)} custom-call(bf16[256,1536]{1,0:T(8,128)(2,1)} %x_hbm.1, s32[6,256]{1,0:T(8,128)} %bitcast.2, f32[6,256]{1,0:T(8,128)} %bitcast.3, bf16[8,1536,512]{2,1,0:T(8,128)(2,1)} %wg_hbm.1, bf16[8,1536,512]{2,1,0:T(8,128)(2,1)} %wu_hbm.1, bf16[8,512,1536]{2,1,0:T(8,128)(2,1)} %wd_hbm.1), custom_call_target="tpu_custom_call" | custom-call | tf_op jit(solution)/shard_map/pallas_call | solution.py:285
  53.6 0.9 %copy.8 = bf16[256,1536]{1,0:T(8,128)(2,1)} copy(bf16[256,1536]{1,0:T(8,128)(2,1)S(1)} %shard_map.64) | data formatting | bytes 1572864

commit v9 on v8

--- a/solution.py
+++ b/solution.py
@@ -73,9 +73,10 @@
         return remote(sgate.at[k], rgate.at[k], gate_sem.at[0], gate_sem.at[1], dests[k])
 
     final = batches - 2
+    ends = [slice(0, d_model - 2 * lanes), slice(d_model - 2 * lanes, d_model)]
 
     def back_copies(k):
-        pieces = halves if k // 2 == final else [slice(0, d_model)]
+        pieces = ends if k // 2 == final else [slice(0, d_model)]
         return [remote(ysend.at[rows(k), cols], yrecv.at[rows(k), cols], back_send.at[0], back_recv.at[0 if k // 2 != final else 1 + h], homes[k])
                 for h, cols in enumerate(pieces)]
 
@@ -258,7 +259,7 @@
     total[...] = x_ref[...].astype(f32) + combine(0, everything)
     for i in (1, batches - 1):
         total[...] += combine(i, everything)
-    for h, cols in enumerate(halves):
+    for h, cols in enumerate(ends):
         wait_back(2 * final, 2, cols, 1 + h)
         out_ref[:, cols] = (total[:, cols] + combine(final, cols)).astype(bf16)
     with scope('sends'):

time: 54.6 us -> 54.5 us (level)
  no operation moved by 1% of the time
where the time goes in v9:
time: 54.5 us; the launch traced here: 54.4 us
  Pallas kernels  53.6 us (98%)
  local copies, waits for them, and re-layouts  0.88 us (2%)
    pallas_call x1, Pallas kernels, device_step(): pl.pallas_call(functools.partial(moe_kernel, groups, cap), out_shape=pltp...  53.6 us

profile of v9, /device:TPU:112, one launch (start us, length us, event | category | flops | bytes accessed | tf_op | source)
XLA Modules:
  0.0 54.4 jit_solution(14916130500441314252)
XLA Ops:
  0.0 53.6 %shard_map.64 = bf16[256,1536]{1,0:T(8,128)(2,1)S(1)} custom-call(bf16[256,1536]{1,0:T(8,128)(2,1)} %x_hbm.1, s32[6,256]{1,0:T(8,128)} %bitcast.2, f32[6,256]{1,0:T(8,128)} %bitcast.3, bf16[8,1536,512]{2,1,0:T(8,128)(2,1)} %wg_hbm.1, bf16[8,1536,512]{2,1,0:T(8,128)(2,1)} %wu_hbm.1, bf16[8,512,1536]{2,1,0:T(8,128)(2,1)} %wd_hbm.1), custom_call_target="tpu_custom_call" | custom-call | tf_op jit(solution)/shard_map/pallas_call | solution.py:286
  53.6 0.9 %copy.8 = bf16[256,1536]{1,0:T(8,128)(2,1)} copy(bf16[256,1536]{1,0:T(8,128)(2,1)S(1)} %shard_map.64) | data formatting | bytes 1572864
